TPU v7x, 32 devices: a whole 2x2x4 slice. The times are simulated.
32 devices in a mesh: row: 8 (over z, x), col: 4 (over y, core).
Axes of the slice: x: 2, y: 2, z: 4, core: 2. Of those that a mesh axis runs over, the one named last changes fastest.
Arguments:
- dense_a: bfloat16 [64, 512, 512], P(('row', 'col')), may hold values from -6 to 6
- dense_b: bfloat16 [64, 512, 512], P(('row', 'col')), may hold values from -0.25 to 0.25
- inner_basis_stack: bfloat16 [64, 2, 512, 128], P(('row', 'col')), may hold values from -0.25 to 0.25
- outer_basis_stack: bfloat16 [64, 2, 512, 128], P(('row', 'col')), may hold values from -1 to 1
- ascent: bfloat16 [32, 4, 2, 128, 128], P(('row', 'col')), may hold values from -0.4375 to 0.4375
- descent: bfloat16 [32, 4, 2, 128, 128], P(('row', 'col')), may hold values from -0.5 to 0.5
- couplings: bfloat16 [32, 2, 4, 128, 128], P(('row', 'col')), may hold values from -0.5 to 0.5
Outputs:
- product_diag: bfloat16 [64, 512, 512], P(('row', 'col'))
All inputs are finite; a program needn't handle non-finite values.
Results may differ from a plain program's by a relative error of at most 0.015.
Values may be sent and summed in bfloat16 or wider, within the bound.
A program may use at most 64 MiB of HBM per device.

v0:
```python
import functools

import jax
import jax.numpy as jnp
from jax import lax
from jax.experimental import pallas as pl
from jax.experimental.pallas import tpu as pltpu
from jax.sharding import PartitionSpec as P

MESH = pl.DeviceIdType.MESH
BF16 = jnp.bfloat16
F32 = jnp.float32
ASC, DESC, COUP = 0, 1, 2


def mm(a, b, ca=1, cb=0):
    return lax.dot_general(
        a.astype(BF16), b.astype(BF16), (((ca,), (cb,)), ((), ())), preferred_element_type=F32
    )


def halves(value):
    high = value.astype(BF16)
    return high, (value - high.astype(F32)).astype(BF16)


def times(value, factor, cb=0):
    if value.dtype == BF16:
        return mm(value, factor, 1, cb)
    rows = value.shape[0]
    both = mm(jnp.concatenate(halves(value), 0), factor, 1, cb)
    return both[:rows] + both[rows:]


def into(factor, value, ca=1):
    if value.dtype == BF16:
        return mm(factor, value, ca, 0)
    columns = value.shape[1]
    both = mm(factor, jnp.concatenate(halves(value), 1), ca, 0)
    return both[:, :columns] + both[:, columns:]


def lift(pair, value):
    return into(pair[0], times(value, pair[1]), 0)


def lower(pair, value):
    return times(into(pair[0], value), pair[1], 1)


def across(first, value, second):
    return times(into(first, value), second)


def tree_kernel(
    levels, columns,
    da_ref, db_ref, inner_ref, outer_ref, asc_ref, desc_ref, coup_ref, o_ref,
    da, db, inner, outer, own_asc, own_desc, own_coup, dense,
    table, f_out, t_out, f_in, t_in, near_leaf, near_up,
    comp, far_in,
    load_sem, gen_send, gen_recv, up_send, up_recv, far_send, far_recv,
):
    pos = lax.axis_index("row") * columns + lax.axis_index("col")
    bit = [pos // 2**i % 2 for i in range(levels)]
    partner = []
    for i in range(levels):
        other = pos + 2**i * (1 - 2 * bit[i])
        partner.append((other // columns, other % columns))

    top = levels - 1
    far = pos + 2**top * (1 - 2 * bit[top])
    cross = far + 2 ** (top - 1) * (1 - 2 * bit[top - 1])
    opposite = (partner[top], (cross // columns, cross % columns))

    low_sum = {}
    for h in range(1, levels + 1):
        total = 0
        for i in range(h):
            total = total + (bit[i] if i == h - 1 else 1 - bit[i])
            low_sum[h, i] = total
    count = {h: low_sum[h, h - 1] for h in range(1, levels + 1)}
    last = {ASC: levels - 2, DESC: levels - 2, COUP: levels}

    barrier = pltpu.get_barrier_semaphore()
    for other in [*partner, opposite[1]]:
        pl.semaphore_signal(barrier, inc=1, device_id=other, device_id_type=MESH)

    loads = [
        pltpu.make_async_copy(src, dst, load_sem.at[n])
        for n, (src, dst) in enumerate([
            (inner_ref, inner),
            (asc_ref.at[0], own_asc),
            (coup_ref.at[0, 0], own_coup),
            (desc_ref.at[0], own_desc),
            (outer_ref, outer),
            (da_ref, da),
            (db_ref, db),
        ])
    ]
    for copy in loads[:4]:
        copy.start()

    def slot(kind, h):
        return table.at[kind, h]

    def own_source(kind):
        return (asc_ref if kind == ASC else desc_ref).at[0, 3]

    def send(kind, h, i, src):
        return pltpu.make_async_remote_copy(
            src_ref=src, dst_ref=slot(kind, h),
            send_sem=gen_send.at[kind, h, i], recv_sem=gen_recv.at[kind, h],
            device_id=partner[i], device_id_type=MESH,
        )

    def wait_slot(kind, h):
        pltpu.make_async_copy(slot(kind, h), slot(kind, h), gen_recv.at[kind, h]).wait()

    def owner_local(kind, h):
        if kind == COUP:
            for n, k in enumerate((0, 3)):
                pltpu.make_async_copy(
                    coup_ref.at[0, 1, k], table.at[COUP, h, n], gen_recv.at[COUP, h]
                ).start()
        else:
            pltpu.make_async_copy(own_source(kind), slot(kind, h), gen_recv.at[kind, h]).start()

    def forwards(k, kinds):
        for kind in kinds:
            for h in range(2, last[kind] + 1):
                if k > h - 1 or (k == 0 and kind != COUP):
                    continue

                @pl.when((count[h] == k) & (low_sum[h, 0] == 0))
                def _(kind=kind, h=h):
                    wait_slot(kind, h)
                    for i in reversed(range(h - 1)):
                        @pl.when(low_sum[h, i] == 0)
                        def _(i=i):
                            send(kind, h, i, slot(kind, h)).start()

    def ready(kind, h):
        if h == 1:
            wait_slot(kind, h)
            return
        waited = low_sum[h, 0] == 0
        if kind != COUP:
            waited = waited & (count[h] > 0)

        @pl.when(jnp.logical_not(waited))
        def _():
            wait_slot(kind, h)

    def up_copy(which, h):
        src, dst = ((f_out, f_in), (t_out, t_in))[which]
        return pltpu.make_async_remote_copy(
            src_ref=src.at[h], dst_ref=dst.at[h],
            send_sem=up_send.at[which, h], recv_sem=up_recv.at[which, h],
            device_id=partner[h], device_id_type=MESH,
        )

    def near(h):
        ready(COUP, h)
        up_copy(0, h - 1).wait()
        pair = slot(COUP, h)
        return across(pair[0], f_in[h - 1], pair[1])

    def far_copy(n):
        return pltpu.make_async_remote_copy(
            src_ref=t_out.at[top - 1], dst_ref=far_in.at[n],
            send_sem=far_send.at[n], recv_sem=far_recv.at[n],
            device_id=opposite[n], device_id_type=MESH,
        )

    def compose(n, left, right, h):
        ready(COUP, h)
        pair = slot(COUP, h)
        for u in range(2):
            comp[n, 0, u] = times(into(own_desc[u, 0], left), pair[0]).astype(BF16)
            high, low = halves(into(own_desc[u, 1], right))
            comp[n, 1, u] = (mm(pair[1], high, 1, 1) + mm(pair[1], low, 1, 1)).astype(BF16)

    pl.semaphore_wait(barrier, levels + 1)

    for h in range(1, levels + 1):
        @pl.when(count[h] == 0)
        def _(h=h):
            for kind in (ASC, DESC, COUP):
                if h > last[kind]:
                    continue
                if kind == COUP:
                    send(kind, h, h - 1, coup_ref.at[0, 1, 1:3]).start()
                else:
                    for i in reversed(range(h)):
                        send(kind, h, i, own_source(kind)).start()
                owner_local(kind, h)

    loads[0].wait()
    for copy in loads[4:]:
        copy.start()
    leaf = [mm(inner[u, 0], inner[u, 1], 0, 0) for u in range(2)]
    loads[1].wait()
    node = lift(own_asc.at[0], leaf[0]) + lift(own_asc.at[1], leaf[1])
    term = lift(own_asc.at[2], node)
    f_out[0] = node.astype(BF16)
    t_out[0] = term.astype(BF16)

    done = 0
    for h in range(top):
        if h > 0:
            ready(ASC, h)
            term = lift(slot(ASC, h), node)
            t_out[h] = term.astype(BF16)
        if h < top - 1:
            up_copy(1, h).start()
        else:
            far_copy(1).start()
            far_copy(0).start()
        if h > 0:
            f_out[h] = node.astype(BF16)
        up_copy(0, h).start()
        if h == 0:
            loads[2].wait()
            near_leaf[0] = across(own_coup[0], leaf[1], own_coup[3])
            near_leaf[1] = across(own_coup[1], leaf[0], own_coup[2])
        if h == 1:
            loads[5].wait()
            loads[6].wait()
        if h in (1, 2):
            dense[h - 1] = mm(da[h - 1], db[h - 1])
        forwards(h + 1, (ASC,))
        forwards(h - 1, (DESC, COUP))
        while done < h - 1:
            done += 1
            near_up[done - 1] = near(done)
        if h < top - 1:
            up_copy(1, h).wait()
            node = term + t_in[h].astype(F32)

    for k in range(top - 1, levels):
        forwards(k, (DESC, COUP))
    loads[3].wait()
    loads[4].wait()
    while done < top - 1:
        done += 1
        near_up[done - 1] = near(done)
    for h in range(1, top):
        ready(DESC, h)
    coupling = near_up[top - 2]
    for h in range(top - 3, -1, -1):
        coupling = near_up[h] + lower(slot(DESC, h) if h else own_desc.at[2], coupling)
    for u in range(2):
        near_leaf[u] += lower(own_desc.at[u], coupling)

    left, right = own_desc[2, 0], own_desc[2, 1]
    for h in range(1, top - 1):
        left, right = times(left, table[DESC, h, 0]), times(right, table[DESC, h, 1])
    compose(0, left, right, top)
    left, right = times(left, table[DESC, top - 1, 0]), times(right, table[DESC, top - 1, 1])
    compose(1, left, right, levels)

    up_copy(0, top - 1).wait()
    for u in range(2):
        near_leaf[u] += mm(mm(comp[0, 0, u], f_in[top - 1]), comp[0, 1, u])
    for n in (0, 1):
        far_copy(n).wait()
    last_inner = (far_in[0].astype(F32) + far_in[1].astype(F32)).astype(BF16)
    for u in range(2):
        value = (near_leaf[u] + mm(mm(comp[1, 0, u], last_inner), comp[1, 1, u])).astype(BF16)
        spread = mm(outer[u, 0], value).astype(BF16)
        o_ref[u] = (dense[u] + mm(spread, outer[u, 1], 1, 1)).astype(BF16)

    for h in range(1, levels + 1):
        for kind in (ASC, DESC, COUP):
            if h > last[kind]:
                continue
            for i in range(h):
                if i == h - 1:
                    sent = count[h] == 0
                else:
                    sent = low_sum[h, i] == 0

                @pl.when(sent)
                def _(kind=kind, h=h, i=i):
                    send(kind, h, i, slot(kind, h)).wait_send()


def shards(levels, columns, dense_a, dense_b, inner, outer, ascent, descent, couplings):
    r = ascent.shape[-1]
    arrays = (dense_a, dense_b, inner, outer, ascent, descent, couplings)
    vmem = pltpu.VMEM
    dma = pltpu.SemaphoreType.DMA
    return pl.pallas_call(
        functools.partial(tree_kernel, levels, columns),
        out_shape=jax.ShapeDtypeStruct(dense_a.shape, BF16),
        in_specs=[pl.BlockSpec(memory_space=pltpu.HBM)] * 7,
        out_specs=pl.BlockSpec(memory_space=pltpu.VMEM),
        scratch_shapes=[
            vmem(dense_a.shape, BF16),
            vmem(dense_b.shape, BF16),
            vmem(inner.shape, BF16),
            vmem(outer.shape, BF16),
            vmem(ascent.shape[1:], BF16),
            vmem(descent.shape[1:], BF16),
            vmem(couplings.shape[2:], BF16),
            vmem(dense_a.shape, F32),
            vmem((3, levels + 1, 2, r, r), BF16),
            vmem((levels, r, r), BF16),
            vmem((levels, r, r), BF16),
            vmem((levels, r, r), BF16),
            vmem((levels, r, r), BF16),
            vmem((2, r, r), F32),
            vmem((levels, r, r), F32),
            vmem((2, 2, 2, r, r), BF16),
            vmem((2, r, r), BF16),
            dma((7,)),
            dma((3, levels + 1, levels)),
            dma((3, levels + 1)),
            dma((2, levels)),
            dma((2, levels)),
            dma((2,)),
            dma((2,)),
        ],
        compiler_params=pltpu.CompilerParams(collective_id=0, has_side_effects=True, vmem_limit_bytes=24 * 2**20),
    )(*(pltpu.with_memory_space_constraint(x, pltpu.HBM) for x in arrays))


def solution(mesh):
    rows, columns = mesh.shape["row"], mesh.shape["col"]
    levels = (rows * columns).bit_length() - 1
    both = ("row", "col")
    placed = (
        P(both, None, None),
        P(both, None, None),
        P(both, None, None, None),
        P(both, None, None, None),
        P(both, None, None, None, None),
        P(both, None, None, None, None),
        P(both, None, None, None, None),
    )
    return jax.shard_map(
        functools.partial(shards, levels, columns),
        mesh=mesh, in_specs=placed, out_specs=P(both, None, None), check_vma=False,
    )
```

profile of v0, /device:TPU:17, one launch (start us, length us, event | category | flops | bytes accessed | tf_op | source)
XLA Modules:
  0.0 22.3 jit_solution(6785995447657029366)
XLA Ops:
  0.0 21.3 %shard_map.73 = bf16[2,512,512]{2,1,0:T(8,128)(2,1)S(1)} custom-call(bf16[2,512,512]{2,1,0:T(8,128)(2,1)} %da_ref.1, bf16[2,512,512]{2,1,0:T(8,128)(2,1)} %db_ref.1, bf16[2,2,512,128]{3,2,1,0:T(8,128)(2,1)} %inner_ref.1, bf16[2,2,512,128]{3,2,1,0:T(8,128)(2,1)} %outer_ref.1, bf16[1,4,2,128,128]{4,3,2,1,0:T(8,128)(2,1)} %asc_ref.1, ...), custom_call_target="tpu_custom_call" | custom-call | tf_op jit(solution)/shard_map/pallas_call | solution.py:293
  21.3 1.0 %copy.9 = bf16[2,512,512]{2,1,0:T(8,128)(2,1)} copy(bf16[2,512,512]{2,1,0:T(8,128)(2,1)S(1)} %shard_map.73) | data formatting | bytes 2097152
where the time goes:
time: 22.4 us; the launch traced here: 22.3 us
  Pallas kernels  21.3 us (95%)
  local copies, waits for them, and re-layouts  0.97 us (4%)
    pallas_call x1, Pallas kernels, shards(): pl.pallas_call(functools.partial(tree_kernel, levels, columns), out_shape...  21.3 us
    unnamed x1, local copies, waits for them, and re-layouts  0.97 us

commit v1 on v0

v1 whole, which is shorter than its diff:
```python
import functools

import jax
import jax.numpy as jnp
from jax import lax
from jax.experimental import pallas as pl
from jax.experimental.pallas import tpu as pltpu
from jax.sharding import PartitionSpec as P

MESH = pl.DeviceIdType.MESH
BF16 = jnp.bfloat16
F32 = jnp.float32
ASC, DESC, COUP, SIB = 0, 1, 2, 3


def mm(a, b, ca=1, cb=0):
    return lax.dot_general(
        a.astype(BF16), b.astype(BF16), (((ca,), (cb,)), ((), ())), preferred_element_type=F32
    )


def rows(values):
    return jnp.concatenate([v.astype(BF16) for v in values], 0)


def cols(values):
    return jnp.concatenate([v.astype(BF16) for v in values], 1)


def split(levels):
    cuts = [0, 1]
    while cuts[-1] < levels:
        cuts.append(min(cuts[-1] + 2, levels))
    return list(zip(cuts[:-1], cuts[1:]))


def tree_kernel(
    levels, columns,
    da_ref, db_ref, inner_ref, outer_ref, asc_ref, desc_ref, coup_ref, o_ref,
    da, db, inner, outer, asc, desc, coup, base, left, right,
    table, t_out, n_out, t_in, n_in,
    load_sem, w_send, w_recv, t_send, t_recv, n_send, n_recv,
):
    pos = lax.axis_index("row") * columns + lax.axis_index("col")
    bit = [pos // 2**i % 2 for i in range(levels)]
    groups = split(levels)
    final = len(groups) - 1
    top = {h: g for g, (lo, hi) in enumerate(groups) for h in range(lo + 1, hi + 1)}
    late = list(range(groups[final][0] + 1, levels + 1))
    r = asc.shape[-1]

    def neighbour(g, f):
        lo, hi = groups[g]
        other = pos
        for i in range(lo, hi):
            if f >> (i - lo) & 1:
                other = other + 2**i * (1 - 2 * bit[i])
        return other // columns, other % columns

    def flips(g):
        lo, hi = groups[g]
        return list(reversed(range(1, 2 ** (hi - lo))))

    def ones(n):
        return pos % 2**n == 2**n - 1

    def owner(h):
        return pos % 2**h == 2 ** (h - 1) - 1

    barrier = pltpu.get_barrier_semaphore()
    greeted = [neighbour(g, f) for g in range(final + 1) for f in flips(g)]
    for other in greeted:
        pl.semaphore_signal(barrier, inc=1, device_id=other, device_id_type=MESH)

    loads = [
        pltpu.make_async_copy(src, dst, load_sem.at[n])
        for n, (src, dst) in enumerate([
            (asc_ref.at[0], asc),
            (inner_ref, inner),
            (coup_ref.at[0], coup),
            (desc_ref.at[0], desc),
            (da_ref, da),
            (db_ref, db),
            (outer_ref, outer),
        ])
    ]
    for copy in loads[:4]:
        copy.start()

    def slot(kind, h):
        return table.at[kind, h]

    def targets(kind, h, g):
        lo, _ = groups[g]
        if g < top[h]:
            return [(f, kind, slot(kind, h)) for f in flips(g)]
        found = []
        for f in flips(g):
            beyond = f >> (h - lo)
            if kind == ASC:
                found.append((f, SIB if beyond else ASC, slot(ASC, h)))
            elif beyond:
                continue
            elif kind == COUP and f >> (h - 1 - lo) & 1:
                found.append((f, COUP, coup.at[1, 1:3]))
            else:
                found.append((f, kind, slot(kind, h)))
        return found

    def copies(kind, h, g):
        return [
            pltpu.make_async_remote_copy(
                src_ref=src, dst_ref=slot(to, h),
                send_sem=w_send.at[kind, h, g, f - 1], recv_sem=w_recv.at[to, h],
                device_id=neighbour(g, f), device_id_type=MESH,
            )
            for f, to, src in targets(kind, h, g)
        ]

    def give(kind, h, gs):
        @pl.when(owner(h))
        def _():
            for g in gs:
                for copy in copies(kind, h, g):
                    copy.start()

    def down(h):
        return list(reversed(range(top[h] + 1)))

    def take(kind, h, who=None):
        waits = jnp.logical_not(owner(h)) if kind != SIB else None
        if who is not None:
            waits = who if waits is None else waits & who

        def body():
            pltpu.make_async_copy(slot(kind, h), slot(kind, h), w_recv.at[kind, h]).wait()
            for g in reversed(range(top[h])):
                @pl.when(ones(groups[g][1]))
                def _(g=g):
                    for copy in copies(kind, h, g):
                        copy.start()

        if waits is None:
            body()
        else:
            pl.when(waits)(body)

    def t_copy(g, f):
        return pltpu.make_async_remote_copy(
            src_ref=t_out.at[g], dst_ref=t_in.at[g, f - 1],
            send_sem=t_send.at[g, f - 1], recv_sem=t_recv.at[g, f - 1],
            device_id=neighbour(g, f), device_id_type=MESH,
        )

    def n_copy(g):
        return pltpu.make_async_remote_copy(
            src_ref=n_out.at[g], dst_ref=n_in.at[g],
            send_sem=n_send.at[g], recv_sem=n_recv.at[g],
            device_id=neighbour(g, 1), device_id_type=MESH,
        )

    sends_next = jnp.logical_not(ones(1))
    relay = ones(1)

    loads[0].wait()
    turned = cols([asc[u, 0].T for u in range(2)])
    lifted_left = mm(asc[2, 0].T, turned).astype(BF16)
    lifted_right = mm(rows([asc[u, 1] for u in range(2)]), asc[2, 1])
    factors = [cols([asc[u, 1], lifted_right[u * r:(u + 1) * r]]) for u in range(2)]
    loads[1].wait()
    for copy in loads[4:]:
        copy.start()
    leaf = [mm(inner[u, 0], inner[u, 1], 0, 0).astype(BF16) for u in range(2)]
    half = rows([mm(leaf[u], factors[u]) for u in range(2)])
    term = mm(lifted_left, half[:, r:])
    t_out[0] = term.astype(BF16)
    n_out[0] = mm(turned, half[:, :r]).astype(BF16)

    loads[2].wait()
    loads[3].wait()
    for h in range(1, levels + 1):
        @pl.when(owner(h))
        def _(h=h):
            table[COUP, h, 0] = coup[1, 0]
            table[COUP, h, 1] = coup[1, 3]
            if h < levels - 1:
                table[ASC, h, 0] = asc[3, 0].T
                table[ASC, h, 1] = asc[3, 1]
                table[DESC, h] = desc[3]

    pl.semaphore_wait(barrier, len(greeted))
    t_copy(0, 1).start()
    n_copy(0).start()
    for h in range(1, levels - 1):
        give(ASC, h, down(h))
    for h in reversed(late):
        give(COUP, h, [final])

    near = [
        mm(mm(coup[0, 0], leaf[1]), coup[0, 3]),
        mm(mm(coup[0, 1], leaf[0]), coup[0, 2]),
    ]
    left_chain = rows([desc[u, 0] for u in range(2)])
    right_chain = rows([desc[u, 1] for u in range(2)])

    t_copy(0, 1).wait()
    node = term + t_in[0, 0].astype(F32)
    crossed = {}
    for g in range(1, final + 1):
        lo, hi = groups[g]
        n_out[g] = node.astype(BF16)
        if hi - lo == 2:
            take(ASC, lo, None if g == 1 else sends_next)
            term = mm(table[ASC, lo, 0], mm(node, table[ASC, lo, 1]))
            t_out[g] = term.astype(BF16)
            for f in flips(g):
                if g < final or f > 1:
                    t_copy(g, f).start()
        n_copy(g).start()
        if g == 1:
            for h in range(1, levels - 1):
                give(COUP, h, down(h))
                give(DESC, h, down(h))
            for h in late:
                give(COUP, h, down(h)[1:])
            loads[4].wait()
            loads[5].wait()
            for u in range(2):
                base[u] = mm(da[u], db[u])
            for h in range(2, levels - 1):
                take(ASC, h, relay)
                if h == groups[top[h]][0] + 1:
                    take(SIB, h, relay)
            for h in late:
                take(COUP, h, ones(groups[final][0]))
        if g < final:
            for f in flips(g):
                t_copy(g, f).wait()
            own = (term + t_in[g, 0].astype(F32)).astype(BF16)
            other = (t_in[g, 1].astype(F32) + t_in[g, 2].astype(F32)).astype(BF16)
            crossed[lo + 2] = other
            take(ASC, lo + 1, sends_next)
            take(SIB, lo + 1, sends_next)
            node = mm(
                cols([table[ASC, lo + 1, 0], table[SIB, lo + 1, 0]]),
                rows([mm(own, table[ASC, lo + 1, 1]), mm(other, table[SIB, lo + 1, 1])]),
            )

    loads[6].wait()
    for h in range(1, levels + 1):
        if h == 2:
            left_chain = mm(left_chain, desc[2, 0]).astype(BF16)
            right_chain = mm(right_chain, desc[2, 1]).astype(BF16)
        elif h > 2:
            take(DESC, h - 2)
            left_chain = mm(left_chain, table[DESC, h - 2, 0]).astype(BF16)
            right_chain = mm(right_chain, table[DESC, h - 2, 1]).astype(BF16)
        if h in late:
            take(COUP, h, jnp.logical_not(ones(groups[final][0])))
        else:
            take(COUP, h)
        before = mm(left_chain, table[COUP, h, 0]).astype(BF16)
        after = mm(table[COUP, h, 1], right_chain, 1, 1).astype(BF16)
        if h in late:
            at = late.index(h) * r
            for u in range(2):
                left[u, :, at:at + r] = mm(outer[u, 0], before[u * r:(u + 1) * r]).astype(BF16)
                right[u, at:at + r, :] = mm(after[:, u * r:(u + 1) * r], outer[u, 1], 1, 1).astype(BF16)
        else:
            if h == groups[top[h]][0] + 1:
                n_copy(top[h]).wait()
                value = n_in[top[h]]
            else:
                value = crossed[h]
            spread = mm(value, after).astype(BF16)
            for u in range(2):
                near[u] += mm(before[u * r:(u + 1) * r], spread[:, u * r:(u + 1) * r])
        if h == late[0] - 1:
            for u in range(2):
                base[u] += mm(mm(outer[u, 0], near[u]), outer[u, 1], 1, 1)

    n_copy(final).wait()
    blocks = [n_in[final]]
    if len(late) == 2:
        for f in (2, 3):
            t_copy(final, f).wait()
        blocks.append((t_in[final, 1].astype(F32) + t_in[final, 2].astype(F32)).astype(BF16))
        zero = jnp.zeros_like(blocks[0])
        blocks = rows([cols([blocks[0], zero]), cols([zero, blocks[1]])])
    else:
        blocks = blocks[0]
    for u in range(2):
        o_ref[u] = (base[u] + mm(mm(left[u], blocks), right[u])).astype(BF16)

    for h in range(1, levels + 1):
        for kind in (ASC, SIB, DESC, COUP):
            if kind != COUP and h > levels - 2:
                continue
            if kind == SIB and (h == 1 or h != groups[top[h]][0] + 1):
                continue
            for g in range(top[h] + 1):
                if g == top[h] and kind == SIB:
                    continue

                @pl.when(owner(h) if g == top[h] else ones(groups[g][1]))
                def _(kind=kind, h=h, g=g):
                    for copy in copies(kind, h, g):
                        copy.wait_send()


def shards(levels, columns, dense_a, dense_b, inner, outer, ascent, descent, couplings):
    r = ascent.shape[-1]
    m = dense_a.shape[-1]
    arrays = (dense_a, dense_b, inner, outer, ascent, descent, couplings)
    vmem = pltpu.VMEM
    dma = pltpu.SemaphoreType.DMA
    groups = split(levels)
    n = len(groups)
    wide = groups[-1][1] - groups[-1][0]
    return pl.pallas_call(
        functools.partial(tree_kernel, levels, columns),
        out_shape=jax.ShapeDtypeStruct(dense_a.shape, BF16),
        in_specs=[pl.BlockSpec(memory_space=pltpu.HBM)] * 7,
        out_specs=pl.BlockSpec(memory_space=pltpu.VMEM),
        scratch_shapes=[
            vmem(dense_a.shape, BF16),
            vmem(dense_b.shape, BF16),
            vmem(inner.shape, BF16),
            vmem(outer.shape, BF16),
            vmem(ascent.shape[1:], BF16),
            vmem(descent.shape[1:], BF16),
            vmem(couplings.shape[1:], BF16),
            vmem(dense_a.shape, F32),
            vmem((2, m, wide * r), BF16),
            vmem((2, wide * r, m), BF16),
            vmem((4, levels + 1, 2, r, r), BF16),
            vmem((n, r, r), BF16),
            vmem((n, r, r), BF16),
            vmem((n, 3, r, r), BF16),
            vmem((n, r, r), BF16),
            dma((7,)),
            dma((4, levels + 1, n, 3)),
            dma((4, levels + 1)),
            dma((n, 3)),
            dma((n, 3)),
            dma((n,)),
            dma((n,)),
        ],
        compiler_params=pltpu.CompilerParams(collective_id=0, has_side_effects=True, vmem_limit_bytes=24 * 2**20),
    )(*(pltpu.with_memory_space_constraint(x, pltpu.HBM) for x in arrays))


def solution(mesh):
    rows_, columns = mesh.shape["row"], mesh.shape["col"]
    levels = (rows_ * columns).bit_length() - 1
    both = ("row", "col")
    placed = (
        P(both, None, None),
        P(both, None, None),
        P(both, None, None, None),
        P(both, None, None, None),
        P(both, None, None, None, None),
        P(both, None, None, None, None),
        P(both, None, None, None, None),
    )
    return jax.shard_map(
        functools.partial(shards, levels, columns),
        mesh=mesh, in_specs=placed, out_specs=P(both, None, None), check_vma=False,
    )
```

time: 22.4 us -> 20.3 us (0.906)
  the two profiles are of different devices: /device:TPU:17 before, /device:TPU:0 now
where the time goes in v1:
time: 20.3 us; the launch traced here: 20.2 us
  Pallas kernels  19.2 us (95%)
  local copies, waits for them, and re-layouts  0.97 us (5%)
    pallas_call x1, Pallas kernels, shards(): pl.pallas_call(functools.partial(tree_kernel, levels, columns), out_shape...  19.2 us
    unnamed x1, local copies, waits for them, and re-layouts  0.97 us

profile of v1, /device:TPU:0, one launch (start us, length us, event | category | flops | bytes accessed | tf_op | source)
XLA Modules:
  0.0 20.2 jit_solution(15387467449721118360)
XLA Ops:
  0.0 19.2 %shard_map.73 = bf16[2,512,512]{2,1,0:T(8,128)(2,1)S(1)} custom-call(bf16[2,512,512]{2,1,0:T(8,128)(2,1)} %da_ref.1, bf16[2,512,512]{2,1,0:T(8,128)(2,1)} %db_ref.1, bf16[2,2,512,128]{3,2,1,0:T(8,128)(2,1)} %inner_ref.1, bf16[2,2,512,128]{3,2,1,0:T(8,128)(2,1)} %outer_ref.1, bf16[1,4,2,128,128]{4,3,2,1,0:T(8,128)(2,1)} %asc_ref.1, ...), custom_call_target="tpu_custom_call" | custom-call | tf_op jit(solution)/shard_map/pallas_call | solution.py:320
  19.2 1.0 %copy.9 = bf16[2,512,512]{2,1,0:T(8,128)(2,1)} copy(bf16[2,512,512]{2,1,0:T(8,128)(2,1)S(1)} %shard_map.73) | data formatting | bytes 2097152

commit v2 on v1

--- a/solution.py
+++ b/solution.py
@@ -34,12 +34,20 @@
     return list(zip(cuts[:-1], cuts[1:]))
 
 
+def kept(levels):
+    groups = split(levels)
+    firsts = [lo + 1 for lo, hi in groups[1:-1] if hi - lo == 2]
+    found = [(COUP, h) for h in range(1, levels + 1)]
+    found += [(kind, h) for h in range(1, levels - 1) for kind in (ASC, DESC)]
+    return found + [(SIB, h) for h in firsts]
+
+
 def tree_kernel(
     levels, columns,
     da_ref, db_ref, inner_ref, outer_ref, asc_ref, desc_ref, coup_ref, o_ref,
     da, db, inner, outer, asc, desc, coup, base, left, right,
-    table, t_out, n_out, t_in, n_in,
-    load_sem, w_send, w_recv, t_send, t_recv, n_send, n_recv,
+    table, t_out, n_out, d_in,
+    load_sem, w_send, w_recv, d_send, d_recv,
 ):
     pos = lax.axis_index("row") * columns + lax.axis_index("col")
     bit = [pos // 2**i % 2 for i in range(levels)]
@@ -47,7 +55,8 @@
     final = len(groups) - 1
     top = {h: g for g, (lo, hi) in enumerate(groups) for h in range(lo + 1, hi + 1)}
     late = list(range(groups[final][0] + 1, levels + 1))
-    r = asc.shape[-1]
+    r, m = asc.shape[-1], da.shape[-1]
+    place = {item: n for n, item in enumerate(kept(levels))}
 
     def neighbour(g, f):
         lo, hi = groups[g]
@@ -88,7 +97,10 @@
         copy.start()
 
     def slot(kind, h):
-        return table.at[kind, h]
+        return table.at[place[kind, h]]
+
+    def weight(kind, h, n):
+        return table[place[kind, h], n]
 
     def targets(kind, h, g):
         lo, _ = groups[g]
@@ -111,7 +123,7 @@
         return [
             pltpu.make_async_remote_copy(
                 src_ref=src, dst_ref=slot(to, h),
-                send_sem=w_send.at[kind, h, g, f - 1], recv_sem=w_recv.at[to, h],
+                send_sem=w_send.at[g], recv_sem=w_recv.at[place[to, h]],
                 device_id=neighbour(g, f), device_id_type=MESH,
             )
             for f, to, src in targets(kind, h, g)
@@ -133,7 +145,7 @@
             waits = who if waits is None else waits & who
 
         def body():
-            pltpu.make_async_copy(slot(kind, h), slot(kind, h), w_recv.at[kind, h]).wait()
+            pltpu.make_async_copy(slot(kind, h), slot(kind, h), w_recv.at[place[kind, h]]).wait()
             for g in reversed(range(top[h])):
                 @pl.when(ones(groups[g][1]))
                 def _(g=g):
@@ -145,19 +157,19 @@
         else:
             pl.when(waits)(body)
 
-    def t_copy(g, f):
+    def arrival(g, f):
+        return 2 * g if f or g == final else 2 * g + 1
+
+    def d_copy(g, f):
         return pltpu.make_async_remote_copy(
-            src_ref=t_out.at[g], dst_ref=t_in.at[g, f - 1],
-            send_sem=t_send.at[g, f - 1], recv_sem=t_recv.at[g, f - 1],
-            device_id=neighbour(g, f), device_id_type=MESH,
+            src_ref=(t_out if f else n_out).at[g], dst_ref=d_in.at[g, f - 1 if g == final and f else f],
+            send_sem=d_send.at[g], recv_sem=d_recv.at[arrival(g, f)],
+            device_id=neighbour(g, f or 1), device_id_type=MESH,
         )
 
-    def n_copy(g):
-        return pltpu.make_async_remote_copy(
-            src_ref=n_out.at[g], dst_ref=n_in.at[g],
-            send_sem=n_send.at[g], recv_sem=n_recv.at[g],
-            device_id=neighbour(g, 1), device_id_type=MESH,
-        )
+    def arrived(g, start, stop):
+        part = d_in.at[g, start:stop]
+        pltpu.make_async_copy(part, part, d_recv.at[arrival(g, start)]).wait()
 
     sends_next = jnp.logical_not(ones(1))
     relay = ones(1)
@@ -181,16 +193,16 @@
     for h in range(1, levels + 1):
         @pl.when(owner(h))
         def _(h=h):
-            table[COUP, h, 0] = coup[1, 0]
-            table[COUP, h, 1] = coup[1, 3]
+            table[place[COUP, h], 0] = coup[1, 0]
+            table[place[COUP, h], 1] = coup[1, 3]
             if h < levels - 1:
-                table[ASC, h, 0] = asc[3, 0].T
-                table[ASC, h, 1] = asc[3, 1]
-                table[DESC, h] = desc[3]
+                table[place[ASC, h], 0] = asc[3, 0].T
+                table[place[ASC, h], 1] = asc[3, 1]
+                table[place[DESC, h]] = desc[3]
 
     pl.semaphore_wait(barrier, len(greeted))
-    t_copy(0, 1).start()
-    n_copy(0).start()
+    d_copy(0, 1).start()
+    d_copy(0, 0).start()
     for h in range(1, levels - 1):
         give(ASC, h, down(h))
     for h in reversed(late):
@@ -203,20 +215,20 @@
     left_chain = rows([desc[u, 0] for u in range(2)])
     right_chain = rows([desc[u, 1] for u in range(2)])
 
-    t_copy(0, 1).wait()
-    node = term + t_in[0, 0].astype(F32)
+    arrived(0, 1, 2)
+    node = term + d_in[0, 1].astype(F32)
     crossed = {}
     for g in range(1, final + 1):
         lo, hi = groups[g]
         n_out[g] = node.astype(BF16)
         if hi - lo == 2:
             take(ASC, lo, None if g == 1 else sends_next)
-            term = mm(table[ASC, lo, 0], mm(node, table[ASC, lo, 1]))
+            term = mm(weight(ASC, lo, 0), mm(node, weight(ASC, lo, 1)))
             t_out[g] = term.astype(BF16)
             for f in flips(g):
                 if g < final or f > 1:
-                    t_copy(g, f).start()
-        n_copy(g).start()
+                    d_copy(g, f).start()
+        d_copy(g, 0).start()
         if g == 1:
             for h in range(1, levels - 1):
                 give(COUP, h, down(h))
@@ -226,24 +238,23 @@
             loads[4].wait()
             loads[5].wait()
             for u in range(2):
-                base[u] = mm(da[u], db[u])
+                base[u * m:(u + 1) * m] = mm(da[u], db[u])
             for h in range(2, levels - 1):
                 take(ASC, h, relay)
-                if h == groups[top[h]][0] + 1:
+                if (SIB, h) in place:
                     take(SIB, h, relay)
             for h in late:
                 take(COUP, h, ones(groups[final][0]))
         if g < final:
-            for f in flips(g):
-                t_copy(g, f).wait()
-            own = (term + t_in[g, 0].astype(F32)).astype(BF16)
-            other = (t_in[g, 1].astype(F32) + t_in[g, 2].astype(F32)).astype(BF16)
+            arrived(g, 1, 4)
+            own = (term + d_in[g, 1].astype(F32)).astype(BF16)
+            other = (d_in[g, 2].astype(F32) + d_in[g, 3].astype(F32)).astype(BF16)
             crossed[lo + 2] = other
             take(ASC, lo + 1, sends_next)
             take(SIB, lo + 1, sends_next)
             node = mm(
-                cols([table[ASC, lo + 1, 0], table[SIB, lo + 1, 0]]),
-                rows([mm(own, table[ASC, lo + 1, 1]), mm(other, table[SIB, lo + 1, 1])]),
+                cols([weight(ASC, lo + 1, 0), weight(SIB, lo + 1, 0)]),
+                rows([mm(own, weight(ASC, lo + 1, 1)), mm(other, weight(SIB, lo + 1, 1))]),
             )
 
     loads[6].wait()
@@ -253,14 +264,14 @@
             right_chain = mm(right_chain, desc[2, 1]).astype(BF16)
         elif h > 2:
             take(DESC, h - 2)
-            left_chain = mm(left_chain, table[DESC, h - 2, 0]).astype(BF16)
-            right_chain = mm(right_chain, table[DESC, h - 2, 1]).astype(BF16)
+            left_chain = mm(left_chain, weight(DESC, h - 2, 0)).astype(BF16)
+            right_chain = mm(right_chain, weight(DESC, h - 2, 1)).astype(BF16)
         if h in late:
             take(COUP, h, jnp.logical_not(ones(groups[final][0])))
         else:
             take(COUP, h)
-        before = mm(left_chain, table[COUP, h, 0]).astype(BF16)
-        after = mm(table[COUP, h, 1], right_chain, 1, 1).astype(BF16)
+        before = mm(left_chain, weight(COUP, h, 0)).astype(BF16)
+        after = mm(weight(COUP, h, 1), right_chain, 1, 1).astype(BF16)
         if h in late:
             at = late.index(h) * r
             for u in range(2):
@@ -268,8 +279,8 @@
                 right[u, at:at + r, :] = mm(after[:, u * r:(u + 1) * r], outer[u, 1], 1, 1).astype(BF16)
         else:
             if h == groups[top[h]][0] + 1:
-                n_copy(top[h]).wait()
-                value = n_in[top[h]]
+                arrived(top[h], 0, 1)
+                value = d_in[top[h], 0]
             else:
                 value = crossed[h]
             spread = mm(value, after).astype(BF16)
@@ -277,35 +288,35 @@
                 near[u] += mm(before[u * r:(u + 1) * r], spread[:, u * r:(u + 1) * r])
         if h == late[0] - 1:
             for u in range(2):
-                base[u] += mm(mm(outer[u, 0], near[u]), outer[u, 1], 1, 1)
-
-    n_copy(final).wait()
-    blocks = [n_in[final]]
+                base[u * m:(u + 1) * m] += mm(mm(outer[u, 0], near[u]), outer[u, 1], 1, 1)
+
+    arrived(final, 0, 1 if len(late) == 1 else 3)
+    blocks = [d_in[final, 0]]
     if len(late) == 2:
-        for f in (2, 3):
-            t_copy(final, f).wait()
-        blocks.append((t_in[final, 1].astype(F32) + t_in[final, 2].astype(F32)).astype(BF16))
+        blocks.append((d_in[final, 1].astype(F32) + d_in[final, 2].astype(F32)).astype(BF16))
         zero = jnp.zeros_like(blocks[0])
         blocks = rows([cols([blocks[0], zero]), cols([zero, blocks[1]])])
     else:
         blocks = blocks[0]
     for u in range(2):
-        o_ref[u] = (base[u] + mm(mm(left[u], blocks), right[u])).astype(BF16)
-
-    for h in range(1, levels + 1):
-        for kind in (ASC, SIB, DESC, COUP):
-            if kind != COUP and h > levels - 2:
-                continue
-            if kind == SIB and (h == 1 or h != groups[top[h]][0] + 1):
-                continue
-            for g in range(top[h] + 1):
-                if g == top[h] and kind == SIB:
-                    continue
-
-                @pl.when(owner(h) if g == top[h] else ones(groups[g][1]))
-                def _(kind=kind, h=h, g=g):
-                    for copy in copies(kind, h, g):
-                        copy.wait_send()
+        o_ref[u] = (base[u * m:(u + 1) * m] + mm(mm(left[u], blocks), right[u])).astype(BF16)
+
+    def settle(ref, sem):
+        pltpu.make_async_copy(ref, ref, sem).wait()
+
+    for g in range(final + 1):
+        sent = 3 if g == final and len(late) == 2 else 1 if g == final else 1 + len(flips(g))
+        settle(d_in.at[g, :sent], d_send.at[g])
+    for k in range(levels + 1):
+        @pl.when(owner(k + 1) if k < levels else ones(levels))
+        def _(k=k):
+            for g in range(final + 1):
+                units = 0
+                for kind, h in place:
+                    if kind != SIB and g == top[h] and k == h - 1 or g < top[h] and k >= groups[g][1]:
+                        units += len(targets(kind, h, g))
+                if units:
+                    settle(base.at[:units * (r * r // m)], w_send.at[g])
 
 
 def shards(levels, columns, dense_a, dense_b, inner, outer, ascent, descent, couplings):
@@ -330,21 +341,18 @@
             vmem(ascent.shape[1:], BF16),
             vmem(descent.shape[1:], BF16),
             vmem(couplings.shape[1:], BF16),
-            vmem(dense_a.shape, F32),
+            vmem((2 * m, m), F32),
             vmem((2, m, wide * r), BF16),
             vmem((2, wide * r, m), BF16),
-            vmem((4, levels + 1, 2, r, r), BF16),
+            vmem((len(kept(levels)), 2, r, r), BF16),
             vmem((n, r, r), BF16),
             vmem((n, r, r), BF16),
-            vmem((n, 3, r, r), BF16),
-            vmem((n, r, r), BF16),
+            vmem((n, 4, r, r), BF16),
             dma((7,)),
-            dma((4, levels + 1, n, 3)),
-            dma((4, levels + 1)),
-            dma((n, 3)),
-            dma((n, 3)),
             dma((n,)),
+            dma((len(kept(levels)),)),
             dma((n,)),
+            dma((2 * n - 1,)),
         ],
         compiler_params=pltpu.CompilerParams(collective_id=0, has_side_effects=True, vmem_limit_bytes=24 * 2**20),
     )(*(pltpu.with_memory_space_constraint(x, pltpu.HBM) for x in arrays))

time: 20.3 us -> 17.7 us (0.87)
  Pallas kernels: 19.2 us -> 16.6 us
    pallas_call x1, Pallas kernels: 19.2 us -> 16.6 us  [shards(): pl.pallas_call(functools.partial(tree_kernel, levels, columns), out_shape...]
where the time goes in v2:
time: 17.7 us; the launch traced here: 17.6 us
  Pallas kernels  16.6 us (94%)
  local copies, waits for them, and re-layouts  0.97 us (5%)
    pallas_call x1, Pallas kernels, shards(): pl.pallas_call(functools.partial(tree_kernel, levels, columns), out_shape...  16.6 us
    unnamed x1, local copies, waits for them, and re-layouts  0.97 us

profile of v2, /device:TPU:0, one launch (start us, length us, event | category | flops | bytes accessed | tf_op | source)
XLA Modules:
  0.0 17.6 jit_solution(10942121189223190883)
XLA Ops:
  0.0 16.6 %shard_map.73 = bf16[2,512,512]{2,1,0:T(8,128)(2,1)S(1)} custom-call(bf16[2,512,512]{2,1,0:T(8,128)(2,1)} %da_ref.1, bf16[2,512,512]{2,1,0:T(8,128)(2,1)} %db_ref.1, bf16[2,2,512,128]{3,2,1,0:T(8,128)(2,1)} %inner_ref.1, bf16[2,2,512,128]{3,2,1,0:T(8,128)(2,1)} %outer_ref.1, bf16[1,4,2,128,128]{4,3,2,1,0:T(8,128)(2,1)} %asc_ref.1, ...), custom_call_target="tpu_custom_call" | custom-call | tf_op jit(solution)/shard_map/pallas_call | solution.py:331
  16.6 1.0 %copy.9 = bf16[2,512,512]{2,1,0:T(8,128)(2,1)} copy(bf16[2,512,512]{2,1,0:T(8,128)(2,1)S(1)} %shard_map.73) | data formatting | bytes 2097152

commit v3 on v2

v3 whole, which is shorter than its diff:
```python
import functools

import jax
import jax.numpy as jnp
from jax import lax
from jax.experimental import pallas as pl
from jax.experimental.pallas import tpu as pltpu
from jax.sharding import PartitionSpec as P

MESH = pl.DeviceIdType.MESH
BF16 = jnp.bfloat16
F32 = jnp.float32
ASC, DESC, COUP, SIB = 0, 1, 2, 3


def mm(a, b, ca=1, cb=0):
    return lax.dot_general(
        a.astype(BF16), b.astype(BF16), (((ca,), (cb,)), ((), ())), preferred_element_type=F32
    )


def rows(values):
    return jnp.concatenate([v.astype(BF16) for v in values], 0)


def cols(values):
    return jnp.concatenate([v.astype(BF16) for v in values], 1)


def split(levels):
    cuts = [0, *range(1, levels + 1, 2)]
    return list(zip(cuts[:-1], cuts[1:]))


def kept(levels):
    groups = split(levels)
    firsts = [lo + 1 for lo, _ in groups[1:-1]]
    found = [(COUP, h) for h in range(1, levels + 1)]
    found += [(kind, h) for h in range(1, levels - 1) for kind in (ASC, DESC)]
    return found + [(SIB, h) for h in firsts]


def tree_kernel(
    levels, columns,
    da_ref, db_ref, inner_ref, outer_ref, asc_ref, desc_ref, coup_ref, o_ref,
    da, db, inner, outer, asc, desc, coup, base,
    table, t_out, n_out, d_in, cross, near,
    load_sem, w_send, w_recv, d_send, d_recv, c_recv,
):
    pos = lax.axis_index("row") * columns + lax.axis_index("col")
    bit = [pos // 2**i % 2 for i in range(levels)]
    groups = split(levels)
    final = len(groups) - 1
    top = {h: g for g, (lo, hi) in enumerate(groups) for h in range(lo + 1, hi + 1)}
    late = list(range(groups[final][0] + 1, levels + 1))
    r, m = asc.shape[-1], da.shape[-1]
    place = {item: n for n, item in enumerate(kept(levels))}

    def neighbour(g, f, core=0):
        lo, hi = groups[g]
        other = pos + core * (1 - 2 * bit[0])
        for i in range(lo, hi):
            if f >> (i - lo) & 1:
                other = other + 2**i * (1 - 2 * bit[i])
        return other // columns, other % columns

    def flips(g):
        lo, hi = groups[g]
        return list(reversed(range(1, 2 ** (hi - lo))))

    def ones(n):
        return pos % 2**n == 2**n - 1

    def owner(h):
        return pos % 2**h == 2 ** (h - 1) - 1

    barrier = pltpu.get_barrier_semaphore()
    hub, side = ones(1), jnp.logical_not(ones(1))
    mate = neighbour(0, 1)
    greeted = [mate, neighbour(final, 3, 1)]
    peers = [neighbour(g, f) for g in range(1, final + 1) for f in flips(g)]

    def greet(others):
        for other in others:
            pl.semaphore_signal(barrier, inc=1, device_id=other, device_id_type=MESH)

    greet(greeted)
    pl.when(hub)(lambda: greet(peers))

    loads = [
        pltpu.make_async_copy(src, dst, load_sem.at[n])
        for n, (src, dst) in enumerate([
            (asc_ref.at[0], asc),
            (inner_ref, inner),
            (coup_ref.at[0], coup),
            (desc_ref.at[0], desc),
            (da_ref, da),
            (db_ref, db),
            (outer_ref, outer),
        ])
    ]
    for copy in loads[:4]:
        copy.start()

    def slot(kind, h):
        return table.at[place[kind, h]]

    def weight(kind, h, n):
        return table[place[kind, h], n]

    def targets(kind, h, g):
        lo, _ = groups[g]
        if g < top[h]:
            return [(f, kind, slot(kind, h)) for f in flips(g)]
        found = []
        for f in flips(g):
            beyond = f >> (h - lo)
            if kind == ASC:
                found.append((f, SIB if beyond else ASC, slot(ASC, h)))
            elif beyond:
                continue
            elif kind == COUP and f >> (h - 1 - lo) & 1:
                found.append((f, COUP, coup.at[1, 1:3]))
            else:
                found.append((f, kind, slot(kind, h)))
        return found

    def copies(kind, h, g):
        return [
            pltpu.make_async_remote_copy(
                src_ref=src, dst_ref=slot(to, h),
                send_sem=w_send.at[g], recv_sem=w_recv.at[place[to, h]],
                device_id=neighbour(g, f), device_id_type=MESH,
            )
            for f, to, src in targets(kind, h, g)
        ]

    def give(kind, h, gs):
        @pl.when(owner(h))
        def _():
            for g in gs:
                for copy in copies(kind, h, g):
                    copy.start()

    def down(kind, h):
        return list(reversed(range(int(kind in (ASC, SIB) and h > 1), top[h] + 1)))

    def take(kind, h, who=None):
        waits = jnp.logical_not(owner(h)) if kind != SIB else None
        if who is not None:
            waits = who if waits is None else waits & who

        def body():
            pltpu.make_async_copy(slot(kind, h), slot(kind, h), w_recv.at[place[kind, h]]).wait()
            for g in [g for g in down(kind, h) if g < top[h]]:
                @pl.when(ones(groups[g][1]))
                def _(g=g):
                    for copy in copies(kind, h, g):
                        copy.start()

        if waits is None:
            body()
        else:
            pl.when(waits)(body)

    def remote(g, src, dst, recv, to):
        return pltpu.make_async_remote_copy(
            src_ref=src, dst_ref=dst, send_sem=d_send.at[g], recv_sem=recv,
            device_id=to, device_id_type=MESH,
        )

    def send_term(g, f):
        remote(g, t_out.at[g], d_in.at[g, f], d_recv.at[g, f], neighbour(g, f)).start()

    def send_value(g):
        h = groups[g][0] + 1
        remote(g, n_out.at[g], cross.at[h], c_recv.at[h], neighbour(g, 1)).start()

    def landed(ref, sem):
        pltpu.make_async_copy(ref, ref, sem).wait()

    def term_in(g, f):
        landed(d_in.at[g, f], d_recv.at[g, f])

    def value_in(h):
        landed(cross.at[h], c_recv.at[h])

    def pass_value(h):
        remote(top[h], cross.at[h], cross.at[h], c_recv.at[h], mate).start()

    def pass_term(g, f):
        remote(g, d_in.at[g, f], d_in.at[g, f], d_recv.at[g, f], mate).start()

    central = ones(groups[final][0])
    ends = bit[levels - 1] == bit[levels - 2]

    loads[0].wait()
    loads[1].wait()
    for copy in loads[4:]:
        copy.start()
    turned = cols([asc[u, 0].T for u in range(2)])
    lifted_left = mm(asc[2, 0].T, turned).astype(BF16)
    lifted_right = mm(rows([asc[u, 1] for u in range(2)]), asc[2, 1])
    factors = [cols([asc[u, 1], lifted_right[u * r:(u + 1) * r]]) for u in range(2)]
    leaf = [mm(inner[u, 0], inner[u, 1], 0, 0).astype(BF16) for u in range(2)]
    half = rows([mm(leaf[u], factors[u]) for u in range(2)])
    t_out[0] = mm(lifted_left, half[:, r:]).astype(BF16)
    n_out[0] = mm(turned, half[:, :r]).astype(BF16)

    loads[2].wait()
    loads[3].wait()
    for h in range(1, levels + 1):
        @pl.when(owner(h))
        def _(h=h):
            table[place[COUP, h], 0] = coup[1, 0]
            table[place[COUP, h], 1] = coup[1, 3]
            if h < levels - 1:
                table[place[ASC, h], 0] = asc[3, 0].T
                table[place[ASC, h], 1] = asc[3, 1]
                table[place[DESC, h]] = desc[3]

    pl.semaphore_wait(barrier, len(greeted) + len(peers) * bit[0])
    pl.when(side)(lambda: send_term(0, 1))
    send_value(0)
    for h in range(1, levels - 1):
        give(ASC, h, down(ASC, h))
    for h in reversed(late):
        give(COUP, h, [final])

    near[0] = mm(mm(coup[0, 0], leaf[1]), coup[0, 3])
    near[1] = mm(mm(coup[0, 1], leaf[0]), coup[0, 2])
    left_chain = rows([desc[u, 0] for u in range(2)])
    right_chain = rows([desc[u, 1] for u in range(2)])

    def dense():
        loads[4].wait()
        loads[5].wait()
        for u in range(2):
            base[u * m:(u + 1) * m] = mm(da[u], db[u])

    def factors(h, left_chain, right_chain):
        before = mm(left_chain, weight(COUP, h, 0)).astype(BF16)
        return before, mm(weight(COUP, h, 1), right_chain, 1, 1).astype(BF16)

    def couple(value, before, after):
        spread = mm(value, after).astype(BF16)
        for u in range(2):
            near[u] += mm(before[u * r:(u + 1) * r], spread[:, u * r:(u + 1) * r])

    def factors(h, left_chain, right_chain):
        before = mm(left_chain, weight(COUP, h, 0)).astype(BF16)
        return before, mm(weight(COUP, h, 1), right_chain, 1, 1).astype(BF16)

    def couple(value, before, after):
        spread = mm(value, after).astype(BF16)
        for u in range(2):
            near[u] += mm(before[u * r:(u + 1) * r], spread[:, u * r:(u + 1) * r])

    @pl.when(hub)
    def _():
        term_in(0, 1)
        node = (t_out[0].astype(F32) + d_in[0, 1].astype(F32)).astype(BF16)
        n_out[1] = node
        take(ASC, 1)
        t_out[1] = mm(weight(ASC, 1, 0), mm(node, weight(ASC, 1, 1))).astype(BF16)
        for f in flips(1):
            send_term(1, f)

    give(COUP, 1, [0])
    give(DESC, 1, [0])
    loads[4].wait()
    loads[5].wait()
    for u in range(2):
        base[u * m:(u + 1) * m] = mm(da[u], db[u])
    pl.when(hub)(lambda: send_value(1))
    for h in range(2, levels - 1):
        give(COUP, h, down(COUP, h))
        give(DESC, h, down(DESC, h))
    for h in late:
        give(COUP, h, down(COUP, h)[1:])

    @pl.when(hub)
    def _():
        for h in range(2, levels - 1):
            take(ASC, h)
            if (SIB, h) in place:
                take(SIB, h)
        for h in late:
            take(COUP, h, central)

    value_in(1)
    take(COUP, 1)
    take(DESC, 1)
    couple(cross[1], *factors(1, left_chain, right_chain))
    left_chain = mm(left_chain, desc[2, 0]).astype(BF16)
    right_chain = mm(right_chain, desc[2, 1]).astype(BF16)

    @pl.when(hub)
    def _():
        for g in range(1, final):
            lo, hi = groups[g]
            up_left = cols([weight(ASC, lo + 1, 0), weight(SIB, lo + 1, 0)])
            up_right = [weight(ASC, lo + 1, 1), weight(SIB, lo + 1, 1)]
            far_left = mm(weight(ASC, hi, 0), up_left).astype(BF16)
            far_right = mm(rows(up_right), weight(ASC, hi, 1))
            both = [cols([far_right[b * r:(b + 1) * r], up_right[b]]) for b in range(2)]
            for f in (1, 2, 3):
                term_in(g, f)
            own = (t_out[g].astype(F32) + d_in[g, 1].astype(F32)).astype(BF16)
            other = (d_in[g, 2].astype(F32) + d_in[g, 3].astype(F32)).astype(BF16)
            half = rows([mm(own, both[0]), mm(other, both[1])])
            t_out[g + 1] = mm(far_left, half[:, :r]).astype(BF16)
            send_term(g + 1, 3)
            send_term(g + 1, 2)
            if g + 1 < final:
                send_term(g + 1, 1)
            else:
                @pl.when(ends)
                def _():
                    remote(
                        final, t_out.at[final], d_in.at[final, 3], d_recv.at[final, 3],
                        neighbour(final, 3, 1),
                    ).start()
            n_out[g + 1] = mm(up_left, half[:, r:]).astype(BF16)
            send_value(g + 1)
            cross[lo + 2] = other
            pass_value(lo + 2)
            value_in(lo + 1)
            pass_value(lo + 1)

    for h in range(2, late[0]):
        take(COUP, h)
        if h > 2:
            if h > 3:
                take(DESC, h - 2)
            left_chain = mm(left_chain, weight(DESC, h - 2, 0)).astype(BF16)
            right_chain = mm(right_chain, weight(DESC, h - 2, 1)).astype(BF16)
        pl.when(side)(functools.partial(value_in, h))
        couple(cross[h], *factors(h, left_chain, right_chain))
    loads[6].wait()
    for h in late:
        take(DESC, h - 2)
    for h in late:
        take(COUP, h, jnp.logical_not(central))
    before, after = {}, {}
    for h in late:
        left_chain = mm(left_chain, weight(DESC, h - 2, 0)).astype(BF16)
        right_chain = mm(right_chain, weight(DESC, h - 2, 1)).astype(BF16)
        before[h], after[h] = factors(h, left_chain, right_chain)
    before = cols([before[h] for h in late])

    @pl.when(hub)
    def _():
        value_in(late[0])
        pass_value(late[0])
        term_in(final, 2)
        pass_term(final, 2)
        term_in(final, 3)
        pl.when(jnp.logical_not(ends))(lambda: pass_term(final, 3))

    @pl.when(side)
    def _():
        value_in(late[0])
        term_in(final, 2)
        term_in(final, 3)

    last = d_in[final, 2].astype(F32) + d_in[final, 3].astype(F32)
    spread = rows([mm(cross[late[0]], after[late[0]]), mm(last, after[late[1]])])
    for u in range(2):
        value = near[u] + mm(before[u * r:(u + 1) * r], spread[:, u * r:(u + 1) * r])
        o_ref[u] = (base[u * m:(u + 1) * m] + mm(mm(outer[u, 0], value), outer[u, 1], 1, 1)).astype(BF16)

    pl.when(side)(lambda: landed(table.at[0], d_send.at[0]))

    @pl.when(hub)
    def _():
        landed(table.at[0, 0], d_send.at[0])
        for g in range(1, final + 1):
            landed(table.at[:3], d_send.at[g])

    for k in range(levels + 1):
        @pl.when(owner(k + 1) if k < levels else ones(levels))
        def _(k=k):
            for g in range(final + 1):
                units = 0
                for kind, h in place:
                    if g not in down(kind, h):
                        continue
                    if kind != SIB and g == top[h] and k == h - 1 or g < top[h] and k >= groups[g][1]:
                        units += len(targets(kind, h, g))
                if units:
                    landed(base.at[:units * (r * r // m)], w_send.at[g])


def shards(levels, columns, dense_a, dense_b, inner, outer, ascent, descent, couplings):
    r = ascent.shape[-1]
    m = dense_a.shape[-1]
    arrays = (dense_a, dense_b, inner, outer, ascent, descent, couplings)
    vmem = pltpu.VMEM
    dma = pltpu.SemaphoreType.DMA
    groups = split(levels)
    n = len(groups)
    return pl.pallas_call(
        functools.partial(tree_kernel, levels, columns),
        out_shape=jax.ShapeDtypeStruct(dense_a.shape, BF16),
        in_specs=[pl.BlockSpec(memory_space=pltpu.HBM)] * 7,
        out_specs=pl.BlockSpec(memory_space=pltpu.VMEM),
        scratch_shapes=[
            vmem(dense_a.shape, BF16),
            vmem(dense_b.shape, BF16),
            vmem(inner.shape, BF16),
            vmem(outer.shape, BF16),
            vmem(ascent.shape[1:], BF16),
            vmem(descent.shape[1:], BF16),
            vmem(couplings.shape[1:], BF16),
            vmem((2 * m, m), F32),
            vmem((len(kept(levels)), 2, r, r), BF16),
            vmem((n, r, r), BF16),
            vmem((n, r, r), BF16),
            vmem((n, 4, r, r), BF16),
            vmem((levels, r, r), BF16),
            vmem((2, r, r), F32),
            dma((7,)),
            dma((n,)),
            dma((len(kept(levels)),)),
            dma((n,)),
            dma((n, 4)),
            dma((levels,)),
        ],
        compiler_params=pltpu.CompilerParams(collective_id=0, has_side_effects=True, vmem_limit_bytes=24 * 2**20),
    )(*(pltpu.with_memory_space_constraint(x, pltpu.HBM) for x in arrays))


def solution(mesh):
    rows_, columns = mesh.shape["row"], mesh.shape["col"]
    levels = (rows_ * columns).bit_length() - 1
    both = ("row", "col")
    placed = (
        P(both, None, None),
        P(both, None, None),
        P(both, None, None, None),
        P(both, None, None, None),
        P(both, None, None, None, None),
        P(both, None, None, None, None),
        P(both, None, None, None, None),
    )
    return jax.shard_map(
        functools.partial(shards, levels, columns),
        mesh=mesh, in_specs=placed, out_specs=P(both, None, None), check_vma=False,
    )
```

time: 17.7 us -> 17 us (0.960)
  Pallas kernels: 16.6 us -> 15.9 us
    pallas_call x1, Pallas kernels: 16.6 us -> 15.9 us  [shards(): pl.pallas_call(functools.partial(tree_kernel, levels, columns), out_shape...]
where the time goes in v3:
time: 17 us; the launch traced here: 16.8 us
  Pallas kernels  15.9 us (94%)
  local copies, waits for them, and re-layouts  0.97 us (6%)
    pallas_call x1, Pallas kernels, shards(): pl.pallas_call(functools.partial(tree_kernel, levels, columns), out_shape...  15.9 us
    unnamed x1, local copies, waits for them, and re-layouts  0.97 us

profile of v3, /device:TPU:0, one launch (start us, length us, event | category | flops | bytes accessed | tf_op | source)
XLA Modules:
  0.0 16.8 jit_solution(12016003498132447134)
XLA Ops:
  0.0 15.9 %shard_map.73 = bf16[2,512,512]{2,1,0:T(8,128)(2,1)S(1)} custom-call(bf16[2,512,512]{2,1,0:T(8,128)(2,1)} %da_ref.1, bf16[2,512,512]{2,1,0:T(8,128)(2,1)} %db_ref.1, bf16[2,2,512,128]{3,2,1,0:T(8,128)(2,1)} %inner_ref.1, bf16[2,2,512,128]{3,2,1,0:T(8,128)(2,1)} %outer_ref.1, bf16[1,4,2,128,128]{4,3,2,1,0:T(8,128)(2,1)} %asc_ref.1, ...), custom_call_target="tpu_custom_call" | custom-call | tf_op jit(solution)/shard_map/pallas_call | solution.py:403
  15.9 1.0 %copy.9 = bf16[2,512,512]{2,1,0:T(8,128)(2,1)} copy(bf16[2,512,512]{2,1,0:T(8,128)(2,1)S(1)} %shard_map.73) | data formatting | bytes 2097152

commit v4 on v3

--- a/solution.py
+++ b/solution.py
@@ -43,7 +43,7 @@
 def tree_kernel(
     levels, columns,
     da_ref, db_ref, inner_ref, outer_ref, asc_ref, desc_ref, coup_ref, o_ref,
-    da, db, inner, outer, asc, desc, coup, base,
+    da, db, inner, outer, asc, desc, coup, base, left, right,
     table, t_out, n_out, d_in, cross, near,
     load_sem, w_send, w_recv, d_send, d_recv, c_recv,
 ):
@@ -66,7 +66,7 @@
 
     def flips(g):
         lo, hi = groups[g]
-        return list(reversed(range(1, 2 ** (hi - lo))))
+        return [f for f in (1, 3, 2) if f < 2 ** (hi - lo)]
 
     def ones(n):
         return pos % 2**n == 2**n - 1
@@ -195,6 +195,12 @@
     ends = bit[levels - 1] == bit[levels - 2]
 
     loads[0].wait()
+    for h in range(1, levels - 1):
+        @pl.when(owner(h))
+        def _(h=h):
+            table[place[ASC, h], 0] = asc[3, 0].T
+            table[place[ASC, h], 1] = asc[3, 1]
+
     loads[1].wait()
     for copy in loads[4:]:
         copy.start()
@@ -207,28 +213,27 @@
     t_out[0] = mm(lifted_left, half[:, r:]).astype(BF16)
     n_out[0] = mm(turned, half[:, :r]).astype(BF16)
 
+    pl.semaphore_wait(barrier, len(greeted) + len(peers) * bit[0])
+    pl.when(side)(lambda: send_term(0, 1))
+    for h in range(1, levels - 1):
+        give(ASC, h, down(ASC, h))
+    send_value(0)
     loads[2].wait()
     loads[3].wait()
-    for h in range(1, levels + 1):
+    for h in reversed(range(1, levels + 1)):
         @pl.when(owner(h))
         def _(h=h):
             table[place[COUP, h], 0] = coup[1, 0]
             table[place[COUP, h], 1] = coup[1, 3]
             if h < levels - 1:
-                table[place[ASC, h], 0] = asc[3, 0].T
-                table[place[ASC, h], 1] = asc[3, 1]
                 table[place[DESC, h]] = desc[3]
 
-    pl.semaphore_wait(barrier, len(greeted) + len(peers) * bit[0])
-    pl.when(side)(lambda: send_term(0, 1))
-    send_value(0)
-    for h in range(1, levels - 1):
-        give(ASC, h, down(ASC, h))
-    for h in reversed(late):
-        give(COUP, h, [final])
-
-    near[0] = mm(mm(coup[0, 0], leaf[1]), coup[0, 3])
-    near[1] = mm(mm(coup[0, 1], leaf[0]), coup[0, 2])
+        if h in late:
+            give(COUP, h, [final])
+        if h == 1:
+            give(COUP, 1, [0])
+            give(DESC, 1, [0])
+
     left_chain = rows([desc[u, 0] for u in range(2)])
     right_chain = rows([desc[u, 1] for u in range(2)])
 
@@ -266,34 +271,37 @@
         for f in flips(1):
             send_term(1, f)
 
-    give(COUP, 1, [0])
-    give(DESC, 1, [0])
-    loads[4].wait()
-    loads[5].wait()
-    for u in range(2):
-        base[u * m:(u + 1) * m] = mm(da[u], db[u])
     pl.when(hub)(lambda: send_value(1))
     for h in range(2, levels - 1):
         give(COUP, h, down(COUP, h))
         give(DESC, h, down(DESC, h))
     for h in late:
         give(COUP, h, down(COUP, h)[1:])
-
-    @pl.when(hub)
-    def _():
-        for h in range(2, levels - 1):
-            take(ASC, h)
-            if (SIB, h) in place:
-                take(SIB, h)
+    loads[4].wait()
+    loads[5].wait()
+    for u in range(2):
+        base[u * m:(u + 1) * m] = mm(da[u], db[u])
+
+    @pl.when(central)
+    def _():
         for h in late:
-            take(COUP, h, central)
-
+            take(COUP, h)
+
+    near[0] = mm(mm(coup[0, 0], leaf[1]), coup[0, 3])
+    near[1] = mm(mm(coup[0, 1], leaf[0]), coup[0, 2])
     value_in(1)
     take(COUP, 1)
     take(DESC, 1)
     couple(cross[1], *factors(1, left_chain, right_chain))
     left_chain = mm(left_chain, desc[2, 0]).astype(BF16)
     right_chain = mm(right_chain, desc[2, 1]).astype(BF16)
+
+    @pl.when(hub)
+    def _():
+        for h in range(2, levels - 1):
+            take(ASC, h)
+            if (SIB, h) in place:
+                take(SIB, h)
 
     @pl.when(hub)
     def _():
@@ -310,17 +318,17 @@
             other = (d_in[g, 2].astype(F32) + d_in[g, 3].astype(F32)).astype(BF16)
             half = rows([mm(own, both[0]), mm(other, both[1])])
             t_out[g + 1] = mm(far_left, half[:, :r]).astype(BF16)
-            send_term(g + 1, 3)
-            send_term(g + 1, 2)
-            if g + 1 < final:
-                send_term(g + 1, 1)
-            else:
+            if g + 1 == final:
                 @pl.when(ends)
                 def _():
                     remote(
                         final, t_out.at[final], d_in.at[final, 3], d_recv.at[final, 3],
                         neighbour(final, 3, 1),
                     ).start()
+            send_term(g + 1, 3)
+            send_term(g + 1, 2)
+            if g + 1 < final:
+                send_term(g + 1, 1)
             n_out[g + 1] = mm(up_left, half[:, r:]).astype(BF16)
             send_value(g + 1)
             cross[lo + 2] = other
@@ -328,26 +336,48 @@
             value_in(lo + 1)
             pass_value(lo + 1)
 
-    for h in range(2, late[0]):
-        take(COUP, h)
+    near_levels = range(2, late[0])
+    loads[6].wait()
+    ready, chains = {}, {}
+    for h in near_levels:
         if h > 2:
             if h > 3:
                 take(DESC, h - 2)
             left_chain = mm(left_chain, weight(DESC, h - 2, 0)).astype(BF16)
             right_chain = mm(right_chain, weight(DESC, h - 2, 1)).astype(BF16)
-        pl.when(side)(functools.partial(value_in, h))
-        couple(cross[h], *factors(h, left_chain, right_chain))
-    loads[6].wait()
-    for h in late:
-        take(DESC, h - 2)
+        chains[h] = left_chain, right_chain
+        if h < late[0] - 1:
+            take(COUP, h)
+            ready[h] = factors(h, *chains[h])
+    if late[0] > 3:
+        take(DESC, late[0] - 2)
+    left_chain = mm(left_chain, weight(DESC, late[0] - 2, 0)).astype(BF16)
+    right_chain = mm(right_chain, weight(DESC, late[0] - 2, 1)).astype(BF16)
+    left_base = [mm(outer[u, 0], left_chain[u * r:(u + 1) * r]).astype(BF16) for u in range(2)]
+    right_base = [mm(outer[u, 1], right_chain[u * r:(u + 1) * r]).astype(BF16) for u in range(2)]
+    take(COUP, late[0] - 1)
+    ready[late[0] - 1] = factors(late[0] - 1, *chains[late[0] - 1])
+
+    @pl.when(side)
+    def _():
+        for h in near_levels:
+            value_in(h)
+
+    for h in near_levels:
+        couple(cross[h], *ready[h])
+    for u in range(2):
+        base[u * m:(u + 1) * m] += mm(mm(outer[u, 0], near[u]), outer[u, 1], 1, 1)
+    take(DESC, late[1] - 2)
     for h in late:
         take(COUP, h, jnp.logical_not(central))
-    before, after = {}, {}
-    for h in late:
-        left_chain = mm(left_chain, weight(DESC, h - 2, 0)).astype(BF16)
-        right_chain = mm(right_chain, weight(DESC, h - 2, 1)).astype(BF16)
-        before[h], after[h] = factors(h, left_chain, right_chain)
-    before = cols([before[h] for h in late])
+    first = cols([weight(COUP, late[0], 0), mm(weight(DESC, late[1] - 2, 0), weight(COUP, late[1], 0))])
+    second = rows([
+        weight(COUP, late[0], 1),
+        mm(weight(COUP, late[1], 1), weight(DESC, late[1] - 2, 1), 1, 1),
+    ])
+    for u in range(2):
+        left[u] = mm(left_base[u], first).astype(BF16)
+        right[u] = mm(second, right_base[u], 1, 1).astype(BF16)
 
     @pl.when(hub)
     def _():
@@ -364,11 +394,11 @@
         term_in(final, 2)
         term_in(final, 3)
 
-    last = d_in[final, 2].astype(F32) + d_in[final, 3].astype(F32)
-    spread = rows([mm(cross[late[0]], after[late[0]]), mm(last, after[late[1]])])
+    last = (d_in[final, 2].astype(F32) + d_in[final, 3].astype(F32)).astype(BF16)
+    zero = jnp.zeros_like(last)
+    blocks = rows([cols([cross[late[0]], zero]), cols([zero, last])])
     for u in range(2):
-        value = near[u] + mm(before[u * r:(u + 1) * r], spread[:, u * r:(u + 1) * r])
-        o_ref[u] = (base[u * m:(u + 1) * m] + mm(mm(outer[u, 0], value), outer[u, 1], 1, 1)).astype(BF16)
+        o_ref[u] = (base[u * m:(u + 1) * m] + mm(mm(left[u], blocks), right[u])).astype(BF16)
 
     pl.when(side)(lambda: landed(table.at[0], d_send.at[0]))
 
@@ -414,6 +444,8 @@
             vmem(descent.shape[1:], BF16),
             vmem(couplings.shape[1:], BF16),
             vmem((2 * m, m), F32),
+            vmem((2, m, 2 * r), BF16),
+            vmem((2, 2 * r, m), BF16),
             vmem((len(kept(levels)), 2, r, r), BF16),
             vmem((n, r, r), BF16),
             vmem((n, r, r), BF16),

time: 17 us -> 15.8 us (0.929)
  Pallas kernels: 15.9 us -> 14.7 us
    pallas_call x1, Pallas kernels: 15.9 us -> 14.7 us  [shards(): pl.pallas_call(functools.partial(tree_kernel, levels, columns), out_shape...]
where the time goes in v4:
time: 15.8 us; the launch traced here: 15.7 us
  Pallas kernels  14.7 us (93%)
  local copies, waits for them, and re-layouts  0.97 us (6%)
    pallas_call x1, Pallas kernels, shards(): pl.pallas_call(functools.partial(tree_kernel, levels, columns), out_shape...  14.7 us
    unnamed x1, local copies, waits for them, and re-layouts  0.97 us

profile of v4, /device:TPU:0, one launch (start us, length us, event | category | flops | bytes accessed | tf_op | source)
XLA Modules:
  0.0 15.7 jit_solution(6241593699119297521)
XLA Ops:
  0.0 14.7 %shard_map.73 = bf16[2,512,512]{2,1,0:T(8,128)(2,1)S(1)} custom-call(bf16[2,512,512]{2,1,0:T(8,128)(2,1)} %da_ref.1, bf16[2,512,512]{2,1,0:T(8,128)(2,1)} %db_ref.1, bf16[2,2,512,128]{3,2,1,0:T(8,128)(2,1)} %inner_ref.1, bf16[2,2,512,128]{3,2,1,0:T(8,128)(2,1)} %outer_ref.1, bf16[1,4,2,128,128]{4,3,2,1,0:T(8,128)(2,1)} %asc_ref.1, ...), custom_call_target="tpu_custom_call" | custom-call | tf_op jit(solution)/shard_map/pallas_call | solution.py:433
  14.7 1.0 %copy.9 = bf16[2,512,512]{2,1,0:T(8,128)(2,1)} copy(bf16[2,512,512]{2,1,0:T(8,128)(2,1)S(1)} %shard_map.73) | data formatting | bytes 2097152

commit v5 on v4

--- a/solution.py
+++ b/solution.py
@@ -45,7 +45,7 @@
     da_ref, db_ref, inner_ref, outer_ref, asc_ref, desc_ref, coup_ref, o_ref,
     da, db, inner, outer, asc, desc, coup, base, left, right,
     table, t_out, n_out, d_in, cross, near,
-    load_sem, w_send, w_recv, d_send, d_recv, c_recv,
+    load_sem, w_send, w_recv, d_send, d_recv, c_recv, told_sem,
 ):
     pos = lax.axis_index("row") * columns + lax.axis_index("col")
     bit = [pos // 2**i % 2 for i in range(levels)]
@@ -77,15 +77,21 @@
     barrier = pltpu.get_barrier_semaphore()
     hub, side = ones(1), jnp.logical_not(ones(1))
     mate = neighbour(0, 1)
-    greeted = [mate, neighbour(final, 3, 1)]
-    peers = [neighbour(g, f) for g in range(1, final + 1) for f in flips(g)]
+    lower = [neighbour(g, f) for g in range(1, final) for f in flips(g)]
+    upper = [neighbour(final, f, 1) for f in flips(final)]
 
     def greet(others):
         for other in others:
             pl.semaphore_signal(barrier, inc=1, device_id=other, device_id_type=MESH)
 
-    greet(greeted)
-    pl.when(hub)(lambda: greet(peers))
+    greet([mate])
+
+    @pl.when(hub)
+    def _():
+        greet(lower)
+        greet(upper)
+
+    pl.when(side)(lambda: greet([neighbour(final, f) for f in flips(final)]))
 
     loads = [
         pltpu.make_async_copy(src, dst, load_sem.at[n])
@@ -169,12 +175,12 @@
             device_id=to, device_id_type=MESH,
         )
 
-    def send_term(g, f):
-        remote(g, t_out.at[g], d_in.at[g, f], d_recv.at[g, f], neighbour(g, f)).start()
-
-    def send_value(g):
+    def send_term(g, f, core=0):
+        remote(g, t_out.at[g], d_in.at[g, f], d_recv.at[g, f], neighbour(g, f, core)).start()
+
+    def send_value(g, core=0):
         h = groups[g][0] + 1
-        remote(g, n_out.at[g], cross.at[h], c_recv.at[h], neighbour(g, 1)).start()
+        remote(g, n_out.at[g], cross.at[h], c_recv.at[h], neighbour(g, 1, core)).start()
 
     def landed(ref, sem):
         pltpu.make_async_copy(ref, ref, sem).wait()
@@ -213,8 +219,19 @@
     t_out[0] = mm(lifted_left, half[:, r:]).astype(BF16)
     n_out[0] = mm(turned, half[:, :r]).astype(BF16)
 
-    pl.semaphore_wait(barrier, len(greeted) + len(peers) * bit[0])
-    pl.when(side)(lambda: send_term(0, 1))
+    def tell_mate():
+        pl.semaphore_signal(told_sem, inc=1, device_id=mate, device_id_type=MESH)
+
+    @pl.when(hub)
+    def _():
+        pl.semaphore_wait(barrier, 1 + len(lower))
+        tell_mate()
+
+    @pl.when(side)
+    def _():
+        pl.semaphore_wait(told_sem, 1)
+        send_term(0, 1)
+
     for h in range(1, levels - 1):
         give(ASC, h, down(ASC, h))
     send_value(0)
@@ -228,29 +245,17 @@
             if h < levels - 1:
                 table[place[DESC, h]] = desc[3]
 
-        if h in late:
-            give(COUP, h, [final])
         if h == 1:
             give(COUP, 1, [0])
             give(DESC, 1, [0])
 
+    @pl.when(side)
+    def _():
+        pl.semaphore_wait(barrier, 1 + 2 * len(upper))
+        tell_mate()
+
     left_chain = rows([desc[u, 0] for u in range(2)])
     right_chain = rows([desc[u, 1] for u in range(2)])
-
-    def dense():
-        loads[4].wait()
-        loads[5].wait()
-        for u in range(2):
-            base[u * m:(u + 1) * m] = mm(da[u], db[u])
-
-    def factors(h, left_chain, right_chain):
-        before = mm(left_chain, weight(COUP, h, 0)).astype(BF16)
-        return before, mm(weight(COUP, h, 1), right_chain, 1, 1).astype(BF16)
-
-    def couple(value, before, after):
-        spread = mm(value, after).astype(BF16)
-        for u in range(2):
-            near[u] += mm(before[u * r:(u + 1) * r], spread[:, u * r:(u + 1) * r])
 
     def factors(h, left_chain, right_chain):
         before = mm(left_chain, weight(COUP, h, 0)).astype(BF16)
@@ -270,6 +275,14 @@
         t_out[1] = mm(weight(ASC, 1, 0), mm(node, weight(ASC, 1, 1))).astype(BF16)
         for f in flips(1):
             send_term(1, f)
+
+    gives_top = owner(late[0]) | owner(late[1])
+
+    @pl.when(gives_top)
+    def _():
+        pl.semaphore_wait(told_sem, 1)
+        for h in reversed(late):
+            give(COUP, h, [final])
 
     pl.when(hub)(lambda: send_value(1))
     for h in range(2, levels - 1):
@@ -319,18 +332,18 @@
             half = rows([mm(own, both[0]), mm(other, both[1])])
             t_out[g + 1] = mm(far_left, half[:, :r]).astype(BF16)
             if g + 1 == final:
-                @pl.when(ends)
-                def _():
-                    remote(
-                        final, t_out.at[final], d_in.at[final, 3], d_recv.at[final, 3],
-                        neighbour(final, 3, 1),
-                    ).start()
-            send_term(g + 1, 3)
-            send_term(g + 1, 2)
-            if g + 1 < final:
-                send_term(g + 1, 1)
+                pl.when(jnp.logical_not(gives_top))(lambda: pl.semaphore_wait(told_sem, 1))
+                pl.when(ends)(lambda: send_term(final, 3, 1))
+                send_term(final, 3)
+                send_term(final, 2)
+                send_term(final, 2, 1)
+            else:
+                for f in flips(g + 1):
+                    send_term(g + 1, f)
             n_out[g + 1] = mm(up_left, half[:, r:]).astype(BF16)
             send_value(g + 1)
+            if g + 1 == final:
+                send_value(final, 1)
             cross[lo + 2] = other
             pass_value(lo + 2)
             value_in(lo + 1)
@@ -379,20 +392,10 @@
         left[u] = mm(left_base[u], first).astype(BF16)
         right[u] = mm(second, right_base[u], 1, 1).astype(BF16)
 
-    @pl.when(hub)
-    def _():
-        value_in(late[0])
-        pass_value(late[0])
-        term_in(final, 2)
-        pass_term(final, 2)
-        term_in(final, 3)
-        pl.when(jnp.logical_not(ends))(lambda: pass_term(final, 3))
-
-    @pl.when(side)
-    def _():
-        value_in(late[0])
-        term_in(final, 2)
-        term_in(final, 3)
+    value_in(late[0])
+    term_in(final, 2)
+    term_in(final, 3)
+    pl.when(hub & jnp.logical_not(ends))(lambda: pass_term(final, 3))
 
     last = (d_in[final, 2].astype(F32) + d_in[final, 3].astype(F32)).astype(BF16)
     zero = jnp.zeros_like(last)
@@ -458,6 +461,7 @@
             dma((n,)),
             dma((n, 4)),
             dma((levels,)),
+            pltpu.SemaphoreType.REGULAR,
         ],
         compiler_params=pltpu.CompilerParams(collective_id=0, has_side_effects=True, vmem_limit_bytes=24 * 2**20),
     )(*(pltpu.with_memory_space_constraint(x, pltpu.HBM) for x in arrays))

time: 15.8 us -> 15.7 us (level)
  no operation moved by 1% of the time
where the time goes in v5:
time: 15.7 us; the launch traced here: 15.6 us
  Pallas kernels  14.6 us (93%)
  local copies, waits for them, and re-layouts  0.97 us (6%)
    pallas_call x1, Pallas kernels, shards(): pl.pallas_call(functools.partial(tree_kernel, levels, columns), out_shape...  14.6 us
    unnamed x1, local copies, waits for them, and re-layouts  0.97 us

profile of v5, /device:TPU:0, one launch (start us, length us, event | category | flops | bytes accessed | tf_op | source)
XLA Modules:
  0.0 15.6 jit_solution(8396344215323796380)
XLA Ops:
  0.0 14.6 %shard_map.73 = bf16[2,512,512]{2,1,0:T(8,128)(2,1)S(1)} custom-call(bf16[2,512,512]{2,1,0:T(8,128)(2,1)} %da_ref.1, bf16[2,512,512]{2,1,0:T(8,128)(2,1)} %db_ref.1, bf16[2,2,512,128]{3,2,1,0:T(8,128)(2,1)} %inner_ref.1, bf16[2,2,512,128]{3,2,1,0:T(8,128)(2,1)} %outer_ref.1, bf16[1,4,2,128,128]{4,3,2,1,0:T(8,128)(2,1)} %asc_ref.1, ...), custom_call_target="tpu_custom_call" | custom-call | tf_op jit(solution)/shard_map/pallas_call | solution.py:436
  14.6 1.0 %copy.9 = bf16[2,512,512]{2,1,0:T(8,128)(2,1)} copy(bf16[2,512,512]{2,1,0:T(8,128)(2,1)S(1)} %shard_map.73) | data formatting | bytes 2097152

commit v6 on v5

--- a/solution.py
+++ b/solution.py
@@ -93,20 +93,14 @@
 
     pl.when(side)(lambda: greet([neighbour(final, f) for f in flips(final)]))
 
-    loads = [
-        pltpu.make_async_copy(src, dst, load_sem.at[n])
-        for n, (src, dst) in enumerate([
-            (asc_ref.at[0], asc),
-            (inner_ref, inner),
-            (coup_ref.at[0], coup),
-            (desc_ref.at[0], desc),
-            (da_ref, da),
-            (db_ref, db),
-            (outer_ref, outer),
-        ])
-    ]
-    for copy in loads[:4]:
-        copy.start()
+    def load(src, dst, n):
+        pltpu.make_async_copy(src, dst, load_sem.at[n]).start()
+
+    def landed(ref, sem):
+        pltpu.make_async_copy(ref, ref, sem).wait()
+
+    load(asc_ref.at[0], asc, 0)
+    load(inner_ref, inner, 1)
 
     def slot(kind, h):
         return table.at[place[kind, h]]
@@ -171,72 +165,86 @@
 
     def remote(g, src, dst, recv, to):
         return pltpu.make_async_remote_copy(
-            src_ref=src, dst_ref=dst, send_sem=d_send.at[g], recv_sem=recv,
+            src_ref=src, dst_ref=dst, send_sem=d_send.at[0], recv_sem=recv,
             device_id=to, device_id_type=MESH,
         )
 
+    def term_sem(g, f):
+        return d_recv.at[g + int(g == final and f == 3)]
+
     def send_term(g, f, core=0):
-        remote(g, t_out.at[g], d_in.at[g, f], d_recv.at[g, f], neighbour(g, f, core)).start()
+        at = f + 4 * core if g == 1 else f
+        remote(g, t_out.at[g], d_in.at[g, at], term_sem(g, f), neighbour(g, f, core)).start()
 
     def send_value(g, core=0):
         h = groups[g][0] + 1
-        remote(g, n_out.at[g], cross.at[h], c_recv.at[h], neighbour(g, 1, core)).start()
-
-    def landed(ref, sem):
-        pltpu.make_async_copy(ref, ref, sem).wait()
+        remote(g, n_out.at[g], cross.at[h], c_recv.at[h - 1], neighbour(g, 1, core)).start()
 
     def term_in(g, f):
-        landed(d_in.at[g, f], d_recv.at[g, f])
+        landed(d_in.at[g, f], term_sem(g, f))
 
     def value_in(h):
-        landed(cross.at[h], c_recv.at[h])
+        landed(cross.at[h], c_recv.at[h - 1])
 
     def pass_value(h):
-        remote(top[h], cross.at[h], cross.at[h], c_recv.at[h], mate).start()
+        remote(top[h], cross.at[h], cross.at[h], c_recv.at[h - 1], mate).start()
 
     def pass_term(g, f):
-        remote(g, d_in.at[g, f], d_in.at[g, f], d_recv.at[g, f], mate).start()
+        remote(g, d_in.at[g, f], d_in.at[g, f], term_sem(g, f), mate).start()
 
     central = ones(groups[final][0])
     ends = bit[levels - 1] == bit[levels - 2]
 
-    loads[0].wait()
+    landed(asc, load_sem.at[0])
     for h in range(1, levels - 1):
         @pl.when(owner(h))
         def _(h=h):
             table[place[ASC, h], 0] = asc[3, 0].T
             table[place[ASC, h], 1] = asc[3, 1]
 
-    loads[1].wait()
-    for copy in loads[4:]:
-        copy.start()
+    def tell_mate():
+        pl.semaphore_signal(told_sem, inc=1, device_id=mate, device_id_type=MESH)
+
+    @pl.when(hub)
+    def _():
+        pl.semaphore_wait(barrier, 1 + len(lower))
+        tell_mate()
+
+    pl.when(side)(lambda: pl.semaphore_wait(told_sem, 1))
+    for h in range(1, levels - 1):
+        give(ASC, h, down(ASC, h))
+    landed(inner, load_sem.at[1])
+    load(coup_ref.at[0], coup, 2)
+    load(desc_ref.at[0], desc, 2)
+    load(da_ref, da, 3)
+    load(db_ref, db, 3)
+    load(outer_ref, outer, 4)
     turned = cols([asc[u, 0].T for u in range(2)])
     lifted_left = mm(asc[2, 0].T, turned).astype(BF16)
     lifted_right = mm(rows([asc[u, 1] for u in range(2)]), asc[2, 1])
     factors = [cols([asc[u, 1], lifted_right[u * r:(u + 1) * r]]) for u in range(2)]
     leaf = [mm(inner[u, 0], inner[u, 1], 0, 0).astype(BF16) for u in range(2)]
     half = rows([mm(leaf[u], factors[u]) for u in range(2)])
-    t_out[0] = mm(lifted_left, half[:, r:]).astype(BF16)
+    term = mm(lifted_left, half[:, r:]).astype(BF16)
     n_out[0] = mm(turned, half[:, :r]).astype(BF16)
-
-    def tell_mate():
-        pl.semaphore_signal(told_sem, inc=1, device_id=mate, device_id_type=MESH)
-
-    @pl.when(hub)
-    def _():
-        pl.semaphore_wait(barrier, 1 + len(lower))
-        tell_mate()
+    t_out[0] = term
+    pl.when(side)(lambda: send_term(0, 1))
+    take(ASC, 1)
+    t_out[1] = mm(weight(ASC, 1, 0), mm(term, weight(ASC, 1, 1))).astype(BF16)
+
+    @pl.when(hub)
+    def _():
+        for f in flips(1):
+            send_term(1, f)
 
     @pl.when(side)
     def _():
-        pl.semaphore_wait(told_sem, 1)
-        send_term(0, 1)
-
-    for h in range(1, levels - 1):
-        give(ASC, h, down(ASC, h))
+        for f in flips(1):
+            send_term(1, f, 1)
+        remote(1, t_out.at[1], d_in.at[1, 4], term_sem(1, 1), mate).start()
+
     send_value(0)
-    loads[2].wait()
-    loads[3].wait()
+    landed(base.at[:16 * r * r // (2 * m)], load_sem.at[2])
     for h in reversed(range(1, levels + 1)):
         @pl.when(owner(h))
         def _(h=h):
@@ -266,16 +274,6 @@
         for u in range(2):
             near[u] += mm(before[u * r:(u + 1) * r], spread[:, u * r:(u + 1) * r])
 
-    @pl.when(hub)
-    def _():
-        term_in(0, 1)
-        node = (t_out[0].astype(F32) + d_in[0, 1].astype(F32)).astype(BF16)
-        n_out[1] = node
-        take(ASC, 1)
-        t_out[1] = mm(weight(ASC, 1, 0), mm(node, weight(ASC, 1, 1))).astype(BF16)
-        for f in flips(1):
-            send_term(1, f)
-
     gives_top = owner(late[0]) | owner(late[1])
 
     @pl.when(gives_top)
@@ -283,6 +281,11 @@
         pl.semaphore_wait(told_sem, 1)
         for h in reversed(late):
             give(COUP, h, [final])
+
+    @pl.when(hub)
+    def _():
+        term_in(0, 1)
+        n_out[1] = (t_out[0].astype(F32) + d_in[0, 1].astype(F32)).astype(BF16)
 
     pl.when(hub)(lambda: send_value(1))
     for h in range(2, levels - 1):
@@ -290,8 +293,7 @@
         give(DESC, h, down(DESC, h))
     for h in late:
         give(COUP, h, down(COUP, h)[1:])
-    loads[4].wait()
-    loads[5].wait()
+    landed(base, load_sem.at[3])
     for u in range(2):
         base[u * m:(u + 1) * m] = mm(da[u], db[u])
 
@@ -325,10 +327,10 @@
             far_left = mm(weight(ASC, hi, 0), up_left).astype(BF16)
             far_right = mm(rows(up_right), weight(ASC, hi, 1))
             both = [cols([far_right[b * r:(b + 1) * r], up_right[b]]) for b in range(2)]
-            for f in (1, 2, 3):
-                term_in(g, f)
-            own = (t_out[g].astype(F32) + d_in[g, 1].astype(F32)).astype(BF16)
-            other = (d_in[g, 2].astype(F32) + d_in[g, 3].astype(F32)).astype(BF16)
+            here, there = ([1], [2, 3]) if g > 1 else ([4, 1, 5], [2, 6, 3, 7])
+            landed(d_in.at[g, 1:1 + len(here + there)], term_sem(g, 1))
+            own = sum((d_in[g, n].astype(F32) for n in here), t_out[g].astype(F32)).astype(BF16)
+            other = sum(d_in[g, n].astype(F32) for n in there).astype(BF16)
             half = rows([mm(own, both[0]), mm(other, both[1])])
             t_out[g + 1] = mm(far_left, half[:, :r]).astype(BF16)
             if g + 1 == final:
@@ -350,7 +352,7 @@
             pass_value(lo + 1)
 
     near_levels = range(2, late[0])
-    loads[6].wait()
+    landed(outer, load_sem.at[4])
     ready, chains = {}, {}
     for h in near_levels:
         if h > 2:
@@ -403,14 +405,9 @@
     for u in range(2):
         o_ref[u] = (base[u * m:(u + 1) * m] + mm(mm(left[u], blocks), right[u])).astype(BF16)
 
-    pl.when(side)(lambda: landed(table.at[0], d_send.at[0]))
-
-    @pl.when(hub)
-    def _():
-        landed(table.at[0, 0], d_send.at[0])
-        for g in range(1, final + 1):
-            landed(table.at[:3], d_send.at[g])
-
+    rows_each = r * r // (2 * m)
+    pl.when(side)(lambda: landed(base.at[:6 * rows_each], d_send.at[0]))
+    pl.when(hub)(lambda: landed(base.at[:(1 + 6 * final) * rows_each], d_send.at[0]))
     for k in range(levels + 1):
         @pl.when(owner(k + 1) if k < levels else ones(levels))
         def _(k=k):
@@ -452,15 +449,15 @@
             vmem((len(kept(levels)), 2, r, r), BF16),
             vmem((n, r, r), BF16),
             vmem((n, r, r), BF16),
-            vmem((n, 4, r, r), BF16),
+            vmem((n, 8, r, r), BF16),
             vmem((levels, r, r), BF16),
             vmem((2, r, r), F32),
-            dma((7,)),
+            dma((5,)),
             dma((n,)),
             dma((len(kept(levels)),)),
-            dma((n,)),
-            dma((n, 4)),
-            dma((levels,)),
+            dma((1,)),
+            dma((n + 1,)),
+            dma((levels - 1,)),
             pltpu.SemaphoreType.REGULAR,
         ],
         compiler_params=pltpu.CompilerParams(collective_id=0, has_side_effects=True, vmem_limit_bytes=24 * 2**20),

time: 15.7 us -> 15.3 us (0.975)
  Pallas kernels: 14.6 us -> 14.1 us
    pallas_call x1, Pallas kernels: 14.6 us -> 14.1 us  [shards(): pl.pallas_call(functools.partial(tree_kernel, levels, columns), out_shape...]
where the time goes in v6:
time: 15.3 us; the launch traced here: 15.1 us
  Pallas kernels  14.1 us (92%)
  local copies, waits for them, and re-layouts  0.97 us (6%)
    pallas_call x1, Pallas kernels, shards(): pl.pallas_call(functools.partial(tree_kernel, levels, columns), out_shape...  14.1 us
    unnamed x1, local copies, waits for them, and re-layouts  0.97 us

profile of v6, /device:TPU:0, one launch (start us, length us, event | category | flops | bytes accessed | tf_op | source)
XLA Modules:
  0.0 15.1 jit_solution(8051624141405659016)
XLA Ops:
  0.0 14.1 %shard_map.73 = bf16[2,512,512]{2,1,0:T(8,128)(2,1)S(1)} custom-call(bf16[2,512,512]{2,1,0:T(8,128)(2,1)} %da_ref.1, bf16[2,512,512]{2,1,0:T(8,128)(2,1)} %db_ref.1, bf16[2,2,512,128]{3,2,1,0:T(8,128)(2,1)} %inner_ref.1, bf16[2,2,512,128]{3,2,1,0:T(8,128)(2,1)} %outer_ref.1, bf16[1,4,2,128,128]{4,3,2,1,0:T(8,128)(2,1)} %asc_ref.1, ...), custom_call_target="tpu_custom_call" | custom-call | tf_op jit(solution)/shard_map/pallas_call | solution.py:433
  14.2 1.0 %copy.9 = bf16[2,512,512]{2,1,0:T(8,128)(2,1)} copy(bf16[2,512,512]{2,1,0:T(8,128)(2,1)S(1)} %shard_map.73) | data formatting | bytes 2097152

commit v7 on v6

--- a/solution.py
+++ b/solution.py
@@ -42,10 +42,10 @@
 
 def tree_kernel(
     levels, columns,
-    da_ref, db_ref, inner_ref, outer_ref, asc_ref, desc_ref, coup_ref, o_ref,
-    da, db, inner, outer, asc, desc, coup, base, left, right,
+    da_ref, db_ref, inner_ref, outer_ref, asc_ref, desc_ref, coup_ref, base, left, right, ends_ref,
+    da, db, inner, outer, asc, desc, coup,
     table, t_out, n_out, d_in, cross, near,
-    load_sem, w_send, w_recv, d_send, d_recv, c_recv, told_sem,
+    load_sem, w_send, w_recv, d_send, d_recv, c_recv, told_sem, pair_sem,
 ):
     pos = lax.axis_index("row") * columns + lax.axis_index("col")
     bit = [pos // 2**i % 2 for i in range(levels)]
@@ -91,7 +91,6 @@
         greet(lower)
         greet(upper)
 
-    pl.when(side)(lambda: greet([neighbour(final, f) for f in flips(final)]))
 
     def load(src, dst, n):
         pltpu.make_async_copy(src, dst, load_sem.at[n]).start()
@@ -234,12 +233,12 @@
 
     @pl.when(hub)
     def _():
-        for f in flips(1):
+        for f in (3, 1, 2):
             send_term(1, f)
 
     @pl.when(side)
     def _():
-        for f in flips(1):
+        for f in (3, 1, 2):
             send_term(1, f, 1)
         remote(1, t_out.at[1], d_in.at[1, 4], term_sem(1, 1), mate).start()
 
@@ -259,7 +258,7 @@
 
     @pl.when(side)
     def _():
-        pl.semaphore_wait(barrier, 1 + 2 * len(upper))
+        pl.semaphore_wait(barrier, 1 + len(upper))
         tell_mate()
 
     left_chain = rows([desc[u, 0] for u in range(2)])
@@ -274,28 +273,29 @@
         for u in range(2):
             near[u] += mm(before[u * r:(u + 1) * r], spread[:, u * r:(u + 1) * r])
 
-    gives_top = owner(late[0]) | owner(late[1])
-
-    @pl.when(gives_top)
+    @pl.when(hub)
     def _():
         pl.semaphore_wait(told_sem, 1)
-        for h in reversed(late):
-            give(COUP, h, [final])
+        for f in flips(final):
+            pl.semaphore_signal(pair_sem, inc=1, device_id=neighbour(final, f), device_id_type=MESH)
+
+    for h in reversed(late):
+        give(COUP, h, [final])
 
     @pl.when(hub)
     def _():
         term_in(0, 1)
         n_out[1] = (t_out[0].astype(F32) + d_in[0, 1].astype(F32)).astype(BF16)
 
+    landed(base, load_sem.at[3])
+    for u in range(2):
+        base[u * m:(u + 1) * m] = mm(da[u], db[u])
     pl.when(hub)(lambda: send_value(1))
     for h in range(2, levels - 1):
         give(COUP, h, down(COUP, h))
         give(DESC, h, down(DESC, h))
     for h in late:
         give(COUP, h, down(COUP, h)[1:])
-    landed(base, load_sem.at[3])
-    for u in range(2):
-        base[u * m:(u + 1) * m] = mm(da[u], db[u])
 
     @pl.when(central)
     def _():
@@ -334,7 +334,7 @@
             half = rows([mm(own, both[0]), mm(other, both[1])])
             t_out[g + 1] = mm(far_left, half[:, :r]).astype(BF16)
             if g + 1 == final:
-                pl.when(jnp.logical_not(gives_top))(lambda: pl.semaphore_wait(told_sem, 1))
+                pl.semaphore_wait(pair_sem, len(upper))
                 pl.when(ends)(lambda: send_term(final, 3, 1))
                 send_term(final, 3)
                 send_term(final, 2)
@@ -399,11 +399,8 @@
     term_in(final, 3)
     pl.when(hub & jnp.logical_not(ends))(lambda: pass_term(final, 3))
 
-    last = (d_in[final, 2].astype(F32) + d_in[final, 3].astype(F32)).astype(BF16)
-    zero = jnp.zeros_like(last)
-    blocks = rows([cols([cross[late[0]], zero]), cols([zero, last])])
-    for u in range(2):
-        o_ref[u] = (base[u * m:(u + 1) * m] + mm(mm(left[u], blocks), right[u])).astype(BF16)
+    ends_ref[0] = cross[late[0]]
+    ends_ref[1] = (d_in[final, 2].astype(F32) + d_in[final, 3].astype(F32)).astype(BF16)
 
     rows_each = r * r // (2 * m)
     pl.when(side)(lambda: landed(base.at[:6 * rows_each], d_send.at[0]))
@@ -422,6 +419,24 @@
                     landed(base.at[:units * (r * r // m)], w_send.at[g])
 
 
+def last_kernel(base, left, right, ends_ref, o_ref, result, sem):
+    m = result.shape[1]
+    near, far = ends_ref[0], ends_ref[1]
+    zero = jnp.zeros_like(far)
+    blocks = rows([cols([near, zero]), cols([zero, far])])
+    spread = [mm(left[u], blocks).astype(BF16) for u in range(2)]
+    copies = []
+    for u in range(2):
+        for n in range(2):
+            part = slice(n * m // 2, (n + 1) * m // 2)
+            start = u * m + n * m // 2
+            result[u, part] = (base[start:start + m // 2] + mm(spread[u][part], right[u])).astype(BF16)
+            copies.append(pltpu.make_async_copy(result.at[u, part], o_ref.at[u, part], sem.at[2 * u + n]))
+            copies[-1].start()
+    for copy in copies:
+        copy.wait()
+
+
 def shards(levels, columns, dense_a, dense_b, inner, outer, ascent, descent, couplings):
     r = ascent.shape[-1]
     m = dense_a.shape[-1]
@@ -430,11 +445,16 @@
     dma = pltpu.SemaphoreType.DMA
     groups = split(levels)
     n = len(groups)
-    return pl.pallas_call(
+    parts = pl.pallas_call(
         functools.partial(tree_kernel, levels, columns),
-        out_shape=jax.ShapeDtypeStruct(dense_a.shape, BF16),
+        out_shape=(
+            jax.ShapeDtypeStruct((2 * m, m), F32),
+            jax.ShapeDtypeStruct((2, m, 2 * r), BF16),
+            jax.ShapeDtypeStruct((2, 2 * r, m), BF16),
+            jax.ShapeDtypeStruct((2, r, r), BF16),
+        ),
         in_specs=[pl.BlockSpec(memory_space=pltpu.HBM)] * 7,
-        out_specs=pl.BlockSpec(memory_space=pltpu.VMEM),
+        out_specs=(pl.BlockSpec(memory_space=pltpu.VMEM),) * 4,
         scratch_shapes=[
             vmem(dense_a.shape, BF16),
             vmem(dense_b.shape, BF16),
@@ -443,9 +463,6 @@
             vmem(ascent.shape[1:], BF16),
             vmem(descent.shape[1:], BF16),
             vmem(couplings.shape[1:], BF16),
-            vmem((2 * m, m), F32),
-            vmem((2, m, 2 * r), BF16),
-            vmem((2, 2 * r, m), BF16),
             vmem((len(kept(levels)), 2, r, r), BF16),
             vmem((n, r, r), BF16),
             vmem((n, r, r), BF16),
@@ -459,9 +476,18 @@
             dma((n + 1,)),
             dma((levels - 1,)),
             pltpu.SemaphoreType.REGULAR,
+            pltpu.SemaphoreType.REGULAR,
         ],
         compiler_params=pltpu.CompilerParams(collective_id=0, has_side_effects=True, vmem_limit_bytes=24 * 2**20),
     )(*(pltpu.with_memory_space_constraint(x, pltpu.HBM) for x in arrays))
+    return pl.pallas_call(
+        last_kernel,
+        out_shape=jax.ShapeDtypeStruct(dense_a.shape, BF16),
+        in_specs=[pl.BlockSpec(memory_space=pltpu.VMEM)] * 4,
+        out_specs=pl.BlockSpec(memory_space=pltpu.HBM),
+        scratch_shapes=[vmem(dense_a.shape, BF16), dma((4,))],
+        compiler_params=pltpu.CompilerParams(vmem_limit_bytes=8 * 2**20),
+    )(*parts)
 
 
 def solution(mesh):

time: 15.3 us -> 15 us (0.980)
  local copies, waits for them, and re-layouts: 0.97 us -> 0 us
  Pallas kernels: 14.1 us -> 14.8 us
    pallas_call x0 -> x1, Pallas kernels: none -> 1.37 us  [shards(): pl.pallas_call(last_kernel, out_shape=jax.ShapeDtypeStruct(dense_a.shape,...]
    unnamed x1 -> x0, local copies, waits for them, and re-layouts: 0.97 us -> none
    pallas_call x1, Pallas kernels: 14.1 us -> 13.5 us  [shards(): pl.pallas_call(functools.partial(tree_kernel, levels, columns), out_shape...]
where the time goes in v7:
time: 15 us; the launch traced here: 14.8 us
  Pallas kernels  14.8 us (99%)
    pallas_call x1, Pallas kernels, shards(): pl.pallas_call(functools.partial(tree_kernel, levels, columns), out_shape...  13.5 us
    pallas_call x1, Pallas kernels, shards(): pl.pallas_call(last_kernel, out_shape=jax.ShapeDtypeStruct(dense_a.shape,...  1.37 us

profile of v7, /device:TPU:0, one launch (start us, length us, event | category | flops | bytes accessed | tf_op | source)
XLA Modules:
  0.0 14.8 jit_solution(9747380938657066748)
XLA Ops:
  0.0 13.5 %shard_map.73 = (f32[1024,512]{1,0:T(8,128)S(1)}, bf16[2,512,256]{2,1,0:T(8,128)(2,1)S(1)}, bf16[2,256,512]{2,1,0:T(8,128)(2,1)S(1)}, bf16[2,128,128]{2,1,0:T(8,128)(2,1)S(1)}) custom-call(bf16[2,512,512]{2,1,0:T(8,128)(2,1)} %da_ref.1, bf16[2,512,512]{2,1,0:T(8,128)(2,1)} %db_ref.1, bf16[2,2,512,128]{3,2,1,0:T(8,128)(2,1)} %inner_ref.1, ...), custom_call_target="tpu_custom_call" | custom-call | tf_op jit(solution)/shard_map/pallas_call | solution.py:448
  13.5 1.4 %shard_map.74 = bf16[2,512,512]{2,1,0:T(8,128)(2,1)} custom-call(f32[1024,512]{1,0:T(8,128)S(1)} %get-tuple-element.9.base, bf16[2,512,256]{2,1,0:T(8,128)(2,1)S(1)} %get-tuple-element.10.left, bf16[2,256,512]{2,1,0:T(8,128)(2,1)S(1)} %get-tuple-element.11.right, bf16[2,128,128]{2,1,0:T(8,128)(2,1)S(1)} %get-tuple-element.12.ends_ref), custom_call_target="tpu_custom_call" | custom-call | tf_op jit(solution)/shard_map/pallas_call | solution.py:483

commit v8 on v7

--- a/solution.py
+++ b/solution.py
@@ -194,20 +194,20 @@
     central = ones(groups[final][0])
     ends = bit[levels - 1] == bit[levels - 2]
 
+    def tell_mate():
+        pl.semaphore_signal(told_sem, inc=1, device_id=mate, device_id_type=MESH)
+
+    @pl.when(hub)
+    def _():
+        pl.semaphore_wait(barrier, 1 + len(lower))
+        tell_mate()
+
     landed(asc, load_sem.at[0])
     for h in range(1, levels - 1):
         @pl.when(owner(h))
         def _(h=h):
             table[place[ASC, h], 0] = asc[3, 0].T
             table[place[ASC, h], 1] = asc[3, 1]
-
-    def tell_mate():
-        pl.semaphore_signal(told_sem, inc=1, device_id=mate, device_id_type=MESH)
-
-    @pl.when(hub)
-    def _():
-        pl.semaphore_wait(barrier, 1 + len(lower))
-        tell_mate()
 
     pl.when(side)(lambda: pl.semaphore_wait(told_sem, 1))
     for h in range(1, levels - 1):
@@ -335,10 +335,16 @@
             t_out[g + 1] = mm(far_left, half[:, :r]).astype(BF16)
             if g + 1 == final:
                 pl.semaphore_wait(pair_sem, len(upper))
-                pl.when(ends)(lambda: send_term(final, 3, 1))
-                send_term(final, 3)
-                send_term(final, 2)
-                send_term(final, 2, 1)
+                @pl.when(ends)
+                def _():
+                    for f, core in ((3, 1), (3, 0), (2, 1), (2, 0)):
+                        send_term(final, f, core)
+
+                @pl.when(jnp.logical_not(ends))
+                def _():
+                    for f, core in ((2, 1), (2, 0), (3, 0)):
+                        send_term(final, f, core)
+
             else:
                 for f in flips(g + 1):
                     send_term(g + 1, f)

time: 15 us -> 15 us (level)
  no operation moved by 1% of the time
where the time goes in v8:
time: 15 us; the launch traced here: 14.9 us
  Pallas kernels  14.9 us (99%)
    pallas_call x1, Pallas kernels, shards(): pl.pallas_call(functools.partial(tree_kernel, levels, columns), out_shape...  13.5 us
    pallas_call x1, Pallas kernels, shards(): pl.pallas_call(last_kernel, out_shape=jax.ShapeDtypeStruct(dense_a.shape,...  1.37 us

profile of v8, /device:TPU:0, one launch (start us, length us, event | category | flops | bytes accessed | tf_op | source)
XLA Modules:
  0.0 14.9 jit_solution(9458540672803555212)
XLA Ops:
  0.0 13.5 %shard_map.73 = (f32[1024,512]{1,0:T(8,128)S(1)}, bf16[2,512,256]{2,1,0:T(8,128)(2,1)S(1)}, bf16[2,256,512]{2,1,0:T(8,128)(2,1)S(1)}, bf16[2,128,128]{2,1,0:T(8,128)(2,1)S(1)}) custom-call(bf16[2,512,512]{2,1,0:T(8,128)(2,1)} %da_ref.1, bf16[2,512,512]{2,1,0:T(8,128)(2,1)} %db_ref.1, bf16[2,2,512,128]{3,2,1,0:T(8,128)(2,1)} %inner_ref.1, ...), custom_call_target="tpu_custom_call" | custom-call | tf_op jit(solution)/shard_map/pallas_call | solution.py:454
  13.5 1.4 %shard_map.74 = bf16[2,512,512]{2,1,0:T(8,128)(2,1)} custom-call(f32[1024,512]{1,0:T(8,128)S(1)} %get-tuple-element.9.base, bf16[2,512,256]{2,1,0:T(8,128)(2,1)S(1)} %get-tuple-element.10.left, bf16[2,256,512]{2,1,0:T(8,128)(2,1)S(1)} %get-tuple-element.11.right, bf16[2,128,128]{2,1,0:T(8,128)(2,1)S(1)} %get-tuple-element.12.ends_ref), custom_call_target="tpu_custom_call" | custom-call | tf_op jit(solution)/shard_map/pallas_call | solution.py:489

commit v9 on v7

--- a/solution.py
+++ b/solution.py
@@ -128,7 +128,7 @@
         return [
             pltpu.make_async_remote_copy(
                 src_ref=src, dst_ref=slot(to, h),
-                send_sem=w_send.at[g], recv_sem=w_recv.at[place[to, h]],
+                send_sem=w_send.at[0], recv_sem=w_recv.at[place[COUP, 1] if (to, h) == (DESC, 1) else place[to, h]],
                 device_id=neighbour(g, f), device_id_type=MESH,
             )
             for f, to, src in targets(kind, h, g)
@@ -305,8 +305,7 @@
     near[0] = mm(mm(coup[0, 0], leaf[1]), coup[0, 3])
     near[1] = mm(mm(coup[0, 1], leaf[0]), coup[0, 2])
     value_in(1)
-    take(COUP, 1)
-    take(DESC, 1)
+    pl.when(hub)(lambda: landed(base.at[:2 * r * r // m], w_recv.at[place[COUP, 1]]))
     couple(cross[1], *factors(1, left_chain, right_chain))
     left_chain = mm(left_chain, desc[2, 0]).astype(BF16)
     right_chain = mm(right_chain, desc[2, 1]).astype(BF16)
@@ -408,15 +407,18 @@
     for k in range(levels + 1):
         @pl.when(owner(k + 1) if k < levels else ones(levels))
         def _(k=k):
+            units = 0
             for g in range(final + 1):
-                units = 0
                 for kind, h in place:
                     if g not in down(kind, h):
                         continue
                     if kind != SIB and g == top[h] and k == h - 1 or g < top[h] and k >= groups[g][1]:
                         units += len(targets(kind, h, g))
-                if units:
-                    landed(base.at[:units * (r * r // m)], w_send.at[g])
+            unit = r * r // m
+            while units:
+                some = min(units, 2 * m // unit)
+                landed(base.at[:some * unit], w_send.at[0])
+                units -= some
 
 
 def last_kernel(base, left, right, ends_ref, o_ref, result, sem):
@@ -427,11 +429,11 @@
     spread = [mm(left[u], blocks).astype(BF16) for u in range(2)]
     copies = []
     for u in range(2):
-        for n in range(2):
-            part = slice(n * m // 2, (n + 1) * m // 2)
-            start = u * m + n * m // 2
-            result[u, part] = (base[start:start + m // 2] + mm(spread[u][part], right[u])).astype(BF16)
-            copies.append(pltpu.make_async_copy(result.at[u, part], o_ref.at[u, part], sem.at[2 * u + n]))
+        for n in range(4):
+            part = slice(n * m // 4, (n + 1) * m // 4)
+            start = u * m + n * m // 4
+            result[u, part] = (base[start:start + m // 4] + mm(spread[u][part], right[u])).astype(BF16)
+            copies.append(pltpu.make_async_copy(result.at[u, part], o_ref.at[u, part], sem.at[4 * u + n]))
             copies[-1].start()
     for copy in copies:
         copy.wait()
@@ -470,7 +472,7 @@
             vmem((levels, r, r), BF16),
             vmem((2, r, r), F32),
             dma((5,)),
-            dma((n,)),
+            dma((1,)),
             dma((len(kept(levels)),)),
             dma((1,)),
             dma((n + 1,)),
@@ -485,7 +487,7 @@
         out_shape=jax.ShapeDtypeStruct(dense_a.shape, BF16),
         in_specs=[pl.BlockSpec(memory_space=pltpu.VMEM)] * 4,
         out_specs=pl.BlockSpec(memory_space=pltpu.HBM),
-        scratch_shapes=[vmem(dense_a.shape, BF16), dma((4,))],
+        scratch_shapes=[vmem(dense_a.shape, BF16), dma((8,))],
         compiler_params=pltpu.CompilerParams(vmem_limit_bytes=8 * 2**20),
     )(*parts)
 

time: 15 us -> 15 us (level)
  no operation moved by 1% of the time
where the time goes in v9:
time: 15 us; the launch traced here: 14.8 us
  Pallas kernels  14.8 us (99%)
    pallas_call x1, Pallas kernels, shards(): pl.pallas_call(functools.partial(tree_kernel, levels, columns), out_shape...  13.4 us
    pallas_call x1, Pallas kernels, shards(): pl.pallas_call(last_kernel, out_shape=jax.ShapeDtypeStruct(dense_a.shape,...  1.37 us

profile of v9, /device:TPU:0, one launch (start us, length us, event | category | flops | bytes accessed | tf_op | source)
XLA Modules:
  0.0 14.8 jit_solution(17970375192718642569)
XLA Ops:
  0.0 13.4 %shard_map.73 = (f32[1024,512]{1,0:T(8,128)S(1)}, bf16[2,512,256]{2,1,0:T(8,128)(2,1)S(1)}, bf16[2,256,512]{2,1,0:T(8,128)(2,1)S(1)}, bf16[2,128,128]{2,1,0:T(8,128)(2,1)S(1)}) custom-call(bf16[2,512,512]{2,1,0:T(8,128)(2,1)} %da_ref.1, bf16[2,512,512]{2,1,0:T(8,128)(2,1)} %db_ref.1, bf16[2,2,512,128]{3,2,1,0:T(8,128)(2,1)} %inner_ref.1, ...), custom_call_target="tpu_custom_call" | custom-call | tf_op jit(solution)/shard_map/pallas_call | solution.py:450
  13.4 1.4 %shard_map.74 = bf16[2,512,512]{2,1,0:T(8,128)(2,1)} custom-call(f32[1024,512]{1,0:T(8,128)S(1)} %get-tuple-element.9.base, bf16[2,512,256]{2,1,0:T(8,128)(2,1)S(1)} %get-tuple-element.10.left, bf16[2,256,512]{2,1,0:T(8,128)(2,1)S(1)} %get-tuple-element.11.right, bf16[2,128,128]{2,1,0:T(8,128)(2,1)S(1)} %get-tuple-element.12.ends_ref), custom_call_target="tpu_custom_call" | custom-call | tf_op jit(solution)/shard_map/pallas_call | solution.py:485

commit v10 on v9

--- a/solution.py
+++ b/solution.py
@@ -335,9 +335,9 @@
             if g + 1 == final:
                 pl.semaphore_wait(pair_sem, len(upper))
                 pl.when(ends)(lambda: send_term(final, 3, 1))
+                send_term(final, 2, 1)
                 send_term(final, 3)
                 send_term(final, 2)
-                send_term(final, 2, 1)
             else:
                 for f in flips(g + 1):
                     send_term(g + 1, f)

time: 15 us -> 15 us (level)
  no operation moved by 1% of the time
where the time goes in v10:
time: 15 us; the launch traced here: 14.8 us
  Pallas kernels  14.8 us (99%)
    pallas_call x1, Pallas kernels, shards(): pl.pallas_call(functools.partial(tree_kernel, levels, columns), out_shape...  13.4 us
    pallas_call x1, Pallas kernels, shards(): pl.pallas_call(last_kernel, out_shape=jax.ShapeDtypeStruct(dense_a.shape,...  1.37 us

profile of v10, /device:TPU:0, one launch (start us, length us, event | category | flops | bytes accessed | tf_op | source)
XLA Modules:
  0.0 14.8 jit_solution(7968142153552513534)
XLA Ops:
  0.0 13.4 %shard_map.73 = (f32[1024,512]{1,0:T(8,128)S(1)}, bf16[2,512,256]{2,1,0:T(8,128)(2,1)S(1)}, bf16[2,256,512]{2,1,0:T(8,128)(2,1)S(1)}, bf16[2,128,128]{2,1,0:T(8,128)(2,1)S(1)}) custom-call(bf16[2,512,512]{2,1,0:T(8,128)(2,1)} %da_ref.1, bf16[2,512,512]{2,1,0:T(8,128)(2,1)} %db_ref.1, bf16[2,2,512,128]{3,2,1,0:T(8,128)(2,1)} %inner_ref.1, ...), custom_call_target="tpu_custom_call" | custom-call | tf_op jit(solution)/shard_map/pallas_call | solution.py:450
  13.4 1.4 %shard_map.74 = bf16[2,512,512]{2,1,0:T(8,128)(2,1)} custom-call(f32[1024,512]{1,0:T(8,128)S(1)} %get-tuple-element.9.base, bf16[2,512,256]{2,1,0:T(8,128)(2,1)S(1)} %get-tuple-element.10.left, bf16[2,256,512]{2,1,0:T(8,128)(2,1)S(1)} %get-tuple-element.11.right, bf16[2,128,128]{2,1,0:T(8,128)(2,1)S(1)} %get-tuple-element.12.ends_ref), custom_call_target="tpu_custom_call" | custom-call | tf_op jit(solution)/shard_map/pallas_call | solution.py:485
